TPU v7x, 256 devices: a whole 4x4x8 slice. The times are simulated.
256 devices in a mesh: gx: 32 (over x, z), gy: 4 (over y), gz: 2 (over core).
Axes of the slice: x: 4, y: 4, z: 8, core: 2. Of those that a mesh axis runs over, the one named last changes fastest.
Arguments:
- coarse_field: float32 [3, 1024, 128, 512], P(None, 'gx', 'gy', 'gz'), may hold values from -6 to 6
- fine_field: float32 [3, 1024, 16, 256], P(None, ('gx', 'gy', 'gz')), may hold values from -6 to 6
- viscosity: float32 [1024, 16, 256], P(('gx', 'gy', 'gz')), may hold values from 0.1 to 1
- corners: int32 [512, 3], replicated, may hold values from 0 to 1016, as said below
- grid_slot: int32 [512], replicated, may hold values from 0 to 1023, as said below
- neighbors: int32 [512, 2], replicated, may hold values from -1 to 511, as said below
Outputs:
- fine_out: float32 [3, 1024, 16, 256], P(None, ('gx', 'gy', 'gz'))
- coarse_out: float32 [3, 1024, 128, 512], P(None, 'gx', 'gy', 'gz')
Inputs may be any that keep to these rules, and one draw needn't show every extreme that they name: Each box is 8 coarse cells on a side, its corner coordinates are multiples of 8, it lies inside the domain and inside one coarse brick of 32 x 32 x 256 cells, and different grids have different boxes. A brick holds either no box or exactly 4 boxes, which share their y and z corners and are grids of one wake. `grid_slot`: different grids have different slots. A grid's slot lies on a device with the same gz index as the brick that holds its box. Every device holds at most 4 grids, some device holds 4 grids in every draw, and all grids of one device lie in one brick. `neighbors`: entry 0 is the grid of the same wake whose box touches the grid's lower x face, entry 1 the one touching its upper x face, or -1 where there is none.
All inputs are finite; a program needn't handle non-finite values.
Results may differ from a plain program's by a relative error of at most 0.00005.
Values sent between devices are 32-bit elements; how exact they have to be, the bound alone decides.
A program may use at most 128 MiB of HBM per device.

v0:
```python
import jax
import jax.numpy as jnp
from jax import lax
from jax.sharding import Mesh
from jax.sharding import PartitionSpec as P

B = 8
F = 16
SLOTS = 4
CUBE = 1024
GX = ("gx_0", "gx_1")
GX_GY_GZ = ("gx_0", "gx_1", "gy", "gz")
GX_GY = ("gx_0", "gx_1", "gy")


step_rate = 0.15


def with_halo(cells, sides, width):
    for axis, dim in sides:
        count = lax.axis_size(axis)
        ends = count - 1
        head = lax.slice_in_dim(cells, 0, width, axis=dim)
        tail = lax.slice_in_dim(cells, cells.shape[dim] - width, cells.shape[dim], axis=dim)
        cells = jnp.concatenate(
            [
                lax.ppermute(tail, axis, [(i, (i + 1) % count) for i in range(ends)]),
                cells,
                lax.ppermute(head, axis, [((i + 1) % count, i) for i in range(ends)]),
            ],
            axis=dim,
        )
    return cells


def joined_along(pieces, dim):
    pieces = jnp.moveaxis(pieces, 0, dim)
    shape = pieces.shape
    return pieces.reshape(*shape[:dim], shape[dim] * shape[dim + 1], *shape[dim + 2 :])


def gather_in_order(array, axes, turns):
    pieces = array
    for k in turns:
        pieces = lax.all_gather(pieces, axes[k])
    done = turns[::-1]
    back = [done.index(k) for k in range(len(axes))]
    pieces = pieces.transpose(*back, *range(len(axes), pieces.ndim))
    return pieces.reshape(-1, *array.shape)


def gathered_by_axis(array, axes, turns, dim):
    return joined_along(gather_in_order(array, axes, turns), dim)


def tables():
    side = B + 2
    fine_index = jnp.arange(F, dtype=jnp.int32)
    coarse_index = jnp.arange(side, dtype=jnp.int32)
    center = fine_index // 2 + 1
    other = jnp.where(fine_index % 2 == 0, center - 1, center + 1)
    tangent = 0.75 * (coarse_index[None, :] == center[:, None]).astype(jnp.float32) + 0.25 * (
        coarse_index[None, :] == other[:, None]
    ).astype(jnp.float32)
    low_side = 0.75 * (coarse_index == 0).astype(jnp.float32) + 0.25 * (coarse_index == 1).astype(
        jnp.float32
    )
    high_side = 0.75 * (coarse_index == side - 1).astype(jnp.float32) + 0.25 * (
        coarse_index == side - 2
    ).astype(jnp.float32)
    return (tangent, low_side, high_side)


def prolong_matrix():
    side = B + 2
    tangent, low_side, high_side = tables()
    blocks = [
        jnp.einsum("a,sb,tc->abcst", low_side, tangent, tangent),
        jnp.einsum("a,sb,tc->abcst", high_side, tangent, tangent),
        jnp.einsum("sa,b,tc->abcst", tangent, low_side, tangent),
        jnp.einsum("sa,b,tc->abcst", tangent, high_side, tangent),
        jnp.einsum("sa,tb,c->abcst", tangent, tangent, low_side),
        jnp.einsum("sa,tb,c->abcst", tangent, tangent, high_side),
    ]
    joined = jnp.concatenate([block.reshape(side**3, F * F) for block in blocks], axis=1)
    return jnp.pad(joined, ((0, CUBE - side**3), (0, 0)))


def advance(volume, visc_cells, ghost_faces, lower_plane, upper_plane):
    components = volume.shape[0]
    slots_here = volume.shape[1]
    cells_edge = volume.shape[2]
    plane_size = volume.shape[3]
    lane_ids = jnp.arange(plane_size, dtype=jnp.int32)
    lane_y = lane_ids // cells_edge
    lane_z = lane_ids % cells_edge
    x_minus = jnp.concatenate([lower_plane[:, :, None], volume[:, :, :-1]], axis=2)
    x_plus = jnp.concatenate([volume[:, :, 1:], upper_plane[:, :, None]], axis=2)
    shape_four = (components, slots_here, cells_edge, cells_edge)
    y_low = jnp.tile(ghost_faces[:, :, 2].reshape(shape_four), (1, 1, 1, cells_edge))
    y_high = jnp.tile(ghost_faces[:, :, 3].reshape(shape_four), (1, 1, 1, cells_edge))
    z_low = jnp.repeat(ghost_faces[:, :, 4].reshape(shape_four), cells_edge, axis=3)
    z_high = jnp.repeat(ghost_faces[:, :, 5].reshape(shape_four), cells_edge, axis=3)
    zero_row = jnp.zeros_like(volume[..., :cells_edge])
    zero_cell = jnp.zeros_like(volume[..., :1])
    y_minus = jnp.where(
        lane_y == 0, y_low, jnp.concatenate([zero_row, volume[..., :-cells_edge]], axis=-1)
    )
    y_plus = jnp.where(
        lane_y == cells_edge - 1,
        y_high,
        jnp.concatenate([volume[..., cells_edge:], zero_row], axis=-1),
    )
    z_minus = jnp.where(lane_z == 0, z_low, jnp.concatenate([zero_cell, volume[..., :-1]], axis=-1))
    z_plus = jnp.where(
        lane_z == cells_edge - 1, z_high, jnp.concatenate([volume[..., 1:], zero_cell], axis=-1)
    )
    neighbor_sum = x_minus + x_plus + y_minus + y_plus + z_minus + z_plus - 6.0 * volume
    return volume + step_rate * visc_cells[None] * neighbor_sum


def row_picker(needed):
    highest = lax.Precision.HIGHEST

    def collect_rows(total_count, piece, start):
        row_ids = jnp.arange(piece.shape[1], dtype=jnp.int32)
        select = (needed[:, None] == row_ids[None, :]).astype(jnp.float32)
        return jnp.einsum("sr,krw->ksw", select, piece, precision=highest)

    return collect_rows


def on_device(coarse_field, fine_field, viscosity, corners, grid_slot, neighbors):
    count_y = lax.axis_size("gy")
    count_z = lax.axis_size("gz")
    index_x = lax.axis_index(GX)
    index_y = lax.axis_index("gy")
    index_z = lax.axis_index("gz")
    brick_x = coarse_field.shape[1]
    brick_y = coarse_field.shape[2]
    brick_z = coarse_field.shape[3]
    grid_total = corners.shape[0]
    grid_ids = jnp.arange(grid_total, dtype=jnp.int32)
    my_device = (index_x * count_y + index_y) * count_z + index_z
    slot_range = jnp.arange(SLOTS, dtype=jnp.int32)
    highest = lax.Precision.HIGHEST
    home_x = corners[:, 0] // brick_x
    home_y = corners[:, 1] // brick_y
    home_z = corners[:, 2] // brick_z
    home_group = home_x * count_y + home_y
    in_brick = (home_x == index_x) & (home_y == index_y) & (home_z == index_z)
    box_x = (corners[:, 0] - home_x * brick_x) // B
    owner_group = grid_slot // SLOTS // count_z
    owner_local = grid_slot % SLOTS
    row_match = in_brick[None, :] & (box_x[None, :] == slot_range[:, None])
    row_present = jnp.any(row_match, axis=1)
    row_grid = jnp.sum(jnp.where(row_match, grid_ids[None, :], 0), axis=1)
    row_corner = corners[row_grid]
    local_y = row_corner[:, 1] - index_y * brick_y
    local_z = row_corner[:, 2] - index_z * brick_z
    anchor_y = jnp.max(jnp.where(row_present, local_y, 0))
    anchor_z = jnp.max(jnp.where(row_present, local_z, 0))
    zero_start = jnp.zeros((), jnp.int32)
    own_slots = my_device * SLOTS + slot_range
    own_match = grid_slot[None, :] == own_slots[:, None]
    slot_active = jnp.any(own_match, axis=1)
    slot_grid = jnp.sum(jnp.where(own_match, grid_ids[None, :], 0), axis=1)
    rimmed = with_halo(coarse_field, ((GX, 1), ("gy", 2), ("gz", 3)), 1)
    side = B + 2
    slab = lax.dynamic_slice(
        rimmed, (zero_start, zero_start, anchor_y, anchor_z), (3, brick_x + 2, side, side)
    )
    cube_list = [
        slab[:, index * B : index * B + side].reshape(3, side**3) for index in range(SLOTS)
    ]
    cubes = jnp.pad(jnp.stack(cube_list, axis=1), ((0, 0), (0, 0), (0, CUBE - side**3)))
    cubes = jnp.where(row_present[None, :, None], cubes, 0.0)
    weights = prolong_matrix()
    payload_width = cubes.shape[-1]
    need_coarse = home_group[slot_grid] * SLOTS + box_x[slot_grid]
    empty_payload = jnp.zeros((3, SLOTS, payload_width), jnp.float32)
    picked = row_picker(need_coarse)(
        empty_payload, lax.all_gather(cubes, GX_GY, axis=1, tiled=True), jnp.int32(0)
    )
    face_values = jnp.dot(
        picked.reshape(3 * SLOTS, CUBE),
        weights,
        precision=highest,
        preferred_element_type=jnp.float32,
    ).reshape(3, SLOTS, 6 * F * F)
    ghost_faces = face_values.reshape(3, SLOTS, 6, F * F)
    slot_near = neighbors[slot_grid]
    low_grid = jnp.maximum(slot_near[:, 0], 0)
    high_grid = jnp.maximum(slot_near[:, 1], 0)
    low_row = owner_group[low_grid] * SLOTS + owner_local[low_grid]
    high_row = owner_group[high_grid] * SLOTS + owner_local[high_grid]
    my_planes = jnp.concatenate([fine_field[:, :, F - 1, :], fine_field[:, :, 0, :]], axis=-1)
    pick_low = row_picker(low_row)
    pick_high = row_picker(high_row)
    empty_plane = jnp.zeros((3, SLOTS, F * F), jnp.float32)
    piece = lax.all_gather(my_planes, GX_GY, axis=1, tiled=True)
    start = jnp.int32(0)
    from_low = pick_low(empty_plane, piece[..., : F * F], start)
    from_high = pick_high(empty_plane, piece[..., F * F :], start)
    has_low = slot_active & (slot_near[:, 0] >= 0)
    has_high = slot_active & (slot_near[:, 1] >= 0)
    lower_plane = jnp.where(has_low[None, :, None], from_low, ghost_faces[:, :, 0])
    upper_plane = jnp.where(has_high[None, :, None], from_high, ghost_faces[:, :, 1])
    advanced = advance(fine_field, viscosity, ghost_faces, lower_plane, upper_plane)
    fine_out = jnp.where(slot_active[None, :, None, None], advanced, 0.0)
    block_means = (
        advanced.reshape(3, SLOTS, B, 2, B, 2, B, 2).mean(axis=(3, 5, 7)).reshape(3, SLOTS, B**3)
    )
    need_average = owner_group[row_grid] * SLOTS + owner_local[row_grid]
    empty_means = jnp.zeros((3, SLOTS, B**3), jnp.float32)
    returned = row_picker(need_average)(
        empty_means, gathered_by_axis(block_means, GX_GY, (0, 1, 2), 1), jnp.int32(0)
    )
    start = (zero_start, zero_start, anchor_y, anchor_z)
    current = lax.dynamic_slice(coarse_field, start, (3, brick_x, B, B))
    new_block = returned.reshape(3, SLOTS * B, B, B)
    x_present = jnp.repeat(row_present, B)
    region = jnp.where(x_present[None, :, None, None], new_block, current)
    coarse_out = lax.dynamic_update_slice(coarse_field, region, start)
    return (fine_out, coarse_out)


def solution(mesh):
    split = Mesh(
        mesh.devices.reshape(4, 8, mesh.shape["gy"], mesh.shape["gz"]), ("gx_0", "gx_1", "gy", "gz")
    )
    in_specs = (
        P(None, GX, "gy", "gz"),
        P(None, GX_GY_GZ, None, None),
        P(GX_GY_GZ, None, None),
        P(),
        P(),
        P(),
    )
    out_specs = (P(None, GX_GY_GZ, None, None), P(None, GX, "gy", "gz"))
    return jax.shard_map(
        on_device, mesh=split, in_specs=in_specs, out_specs=out_specs, check_vma=False
    )
```

profile of v0, /device:TPU:8, one launch (start us, length us, event | category | flops | bytes accessed | tf_op | source)
XLA Modules:
  0.0 432.8 jit_solution(7089443190861817693)
XLA Ops:
  10.9 3.8 collective-permute-start
  16.0 3.7 copy.142
  29.2 3.5 collective-permute-start.2
  42.8 3.1 copy.145
  45.9 3.1 copy.144
  57.4 3.1 copy.147
  60.5 3.1 copy.146
  75.3 6.3 %multiply_bitcast_fusion.4 = (f32[10,10,10,16,16]{4,3,2,1,0:T(8,128)}, f32[10,10,10,16,16]{4,3,2,1,0:T(8,128)}) fusion(f32[16,10,10]{0,1,2:T(8,128)S(1)} %get-tuple-element.46, f32[16,10]{0,1:T(8,128)S(1)} %select_add_fusion, f32[16,10,10]{0,1,2:T(8,128)S(1)} %get-tuple-element.47), kind=kLoop, calls=%fused_computation.14 | loop fusion | flops 512000 | bytes 2061440 | tf_op jit(solution)/shard_map/a,sb,tc->abcst/transpose | solution.py:79
  81.5 6.0 %reshape.295 = f32[1000,256]{1,0:T(8,128)S(1)} reshape(f32[10,10,10,16,16]{4,3,2,1,0:T(8,128)} %get-tuple-element.44) | data formatting | bytes 2048000 | tf_op jit(solution)/shard_map/reshape | solution.py:85
  87.5 6.0 %reshape.294 = f32[1000,256]{1,0:T(8,128)S(1)} reshape(f32[10,10,10,16,16]{4,3,2,1,0:T(8,128)} %get-tuple-element.45) | data formatting | bytes 2048000 | tf_op jit(solution)/shard_map/reshape | solution.py:85
  93.5 12.8 %multiply_bitcast_fusion = (f32[10,10,10,16,16]{4,3,2,1,0:T(8,128)}, f32[10,10,10,16,16]{4,3,1,2,0:T(8,128)}, f32[10,10,10,16,16]{4,3,1,2,0:T(8,128)}, f32[10,10,10,16,16]{4,3,2,1,0:T(8,128)}) fusion(f32[10,16,10]{1,0,2:T(8,128)S(1)} %get-tuple-element.42, f32[16,10]{0,1:T(8,128)S(1)} %select_add_fusion, f32[10,16,10]{1,0,2:T(8,128)S(1)} %get-tuple-element.43), kind=kLoop, calls=%fused_computation.10 | loop fusion | flops 512000 | bytes 4109440 | tf_op jit(solution)/shard_map/sa,tb,c->abcst/transpose | solution.py:83
  106.3 6.0 %reshape.299 = f32[1000,256]{1,0:T(8,128)S(1)} reshape(f32[10,10,10,16,16]{4,3,2,1,0:T(8,128)} %get-tuple-element.32) | data formatting | bytes 2048000 | tf_op jit(solution)/shard_map/reshape | solution.py:85
  112.4 6.9 %reshape.298 = f32[1000,256]{1,0:T(8,128)} reshape(f32[10,10,10,16,16]{4,3,2,1,0:T(8,128)} %get-tuple-element.41) | data formatting | bytes 2048000 | tf_op jit(solution)/shard_map/reshape | solution.py:85
  119.2 7.6 %copy.158 = f32[10,10,10,16,16]{4,3,2,1,0:T(8,128)} copy(f32[10,10,10,16,16]{4,3,1,2,0:T(8,128)} %get-tuple-element.33) | data formatting | bytes 2048000 | tf_op jit(solution)/shard_map/sa,b,tc->abcst/transpose | solution.py:81
  126.8 6.8 %reshape.297 = f32[1000,256]{1,0:T(8,128)} reshape(f32[10,10,10,16,16]{4,3,2,1,0:T(8,128)} %copy.158) | data formatting | bytes 2048000 | tf_op jit(solution)/shard_map/reshape | solution.py:85
  133.6 7.5 %copy.157 = f32[10,10,10,16,16]{4,3,2,1,0:T(8,128)} copy(f32[10,10,10,16,16]{4,3,1,2,0:T(8,128)} %get-tuple-element.40) | data formatting | bytes 2048000 | tf_op jit(solution)/shard_map/sa,b,tc->abcst/transpose | solution.py:80
  141.2 6.8 %reshape.296 = f32[1000,256]{1,0:T(8,128)} reshape(f32[10,10,10,16,16]{4,3,2,1,0:T(8,128)} %copy.157) | data formatting | bytes 2048000 | tf_op jit(solution)/shard_map/reshape | solution.py:85
  150.3 3.0 pad_bitcast_fusion
  153.3 6.8 %copy.159 = f32[1536,1024]{1,0:T(8,128)} copy(f32[1536,1024]{0,1:T(8,128)} %pad_bitcast_fusion) | data formatting | bytes 12582912 | tf_op jit(solution)/shard_map/dot_general | solution.py:185
  163.3 4.2 fusion.75
  167.6 88.9 %all-gather.8.cloned.1.call-done = f32[3,512,1024]{2,0,1:T(4,128)} async-done(((f32[3,4,1024]{2,0,1:T(4,128)}), f32[3,512,1024]{2,0,1:T(4,128)}) %all-gather.8.cloned.1.call-update) | async-done | bytes 6291472 | tf_op jit(solution)/shard_map/all_gather | solution.py:183
  256.4 8.8 %fusion.6 = f32[3,4,1024,1]{2,1,3,0:T(4,128)S(1)} fusion(f32[3,512,1024]{2,0,1:T(4,128)} %all-gather.8.cloned.1.call-done, s32[4]{0:T(128)S(1)} %multiply_add_fusion.3), kind=kOutput, calls=%fused_computation.32 | convolution fusion | flops 75499520 | bytes 6340624 | tf_op jit(solution)/shard_map/sr,krw->ksw/dot_general | solution.py:128
  265.3 8.0 %fusion.86 = f32[3,4,6,256]{3,1,2,0:T(4,128)S(1)} fusion(f32[3,4,1024,1]{2,1,3,0:T(4,128)S(1)} %fusion.6, f32[6,256,1024,1]{2,1,0,3:T(8,128)} %bitcast.114), kind=kOutput, calls=%fused_computation.206 | convolution fusion | flops 226492416 | bytes 6414336 | tf_op jit(solution)/shard_map/dot_general | solution.py:185
  285.2 4.0 copy.164
  289.1 7.6 %reduce_sum.35 = f32[3,4,8,8,8]{1,4,3,2,0:T(8,128)S(1)} reduce(f32[3,4,8,2,8,2,8,2]{1,7,6,5,4,3,2,0:T(2,128)} %bitcast.115, f32[]{:T(128)} %constant.191.clone.1), dimensions={3,5,7}, to_apply=%region_6.7 | reduce | flops 43008 | bytes 221188 | tf_op jit(solution)/shard_map/reduce_sum | solution.py:212
  297.1 12.0 %all_gather.23 = f32[4,3,4,512]{3,2,1,0:T(4,128)S(1)} all-gather(f32[1,3,4,512]{3,2,1,0:T(4,128)S(1)} %copy.165), channel_id=1, replica_groups=mesh['gx_0'=4,'gx_1'=8,'gy'=4,'gz'=2] {'gx_0'}, dimensions={0}, use_global_device_ids=true | all-gather | bytes 122880 | tf_op jit(solution)/shard_map/all_gather | solution.py:45
  309.1 28.3 %all-gather = f32[32,3,4,512]{3,2,1,0:T(4,128)} all-gather(f32[4,3,4,512]{3,2,1,0:T(4,128)S(1)} %all_gather.23), channel_id=2, replica_groups=mesh['gx_0'=4,'gx_1'=8,'gy'=4,'gz'=2] {'gx_1'}, dimensions={0}, use_global_device_ids=true | all-gather | bytes 884736 | tf_op jit(solution)/shard_map/all_gather | solution.py:45
  341.6 34.0 %all-gather.10.cloned.1.call-done = f32[32,4,3,4,512]{4,3,2,1,0:T(4,128)} async-done(((f32[8,4,3,4,512]{4,3,2,1,0:T(4,128)}), f32[32,4,3,4,512]{4,3,2,1,0:T(4,128)}) %all-gather.10.cloned.1.call-update) | async-done | bytes 3145744 | tf_op jit(solution)/shard_map/all_gather | solution.py:45
  375.6 3.7 copy.199
  379.3 3.7 copy.170
  383.0 3.2 reshape.304
  389.3 36.5 %dynamic_update_slice.3 = f32[3,32,32,256]{3,2,1,0:T(8,128)} dynamic-update-slice(f32[3,32,32,256]{3,2,1,0:T(8,128)} %copy-done, f32[3,32,8,8]{3,2,1,0:T(8,128)S(1)} %dynamic-slice_select_fusion, s32[]{:T(128)} %constant.177.clone.1, s32[]{:T(128)} %constant.177.clone.1, s32[]{:T(128)S(6)} %select_n.236, s32[]{:T(128)S(6)} %select_n.237) | dynamic-update-slice | bytes 49156 | tf_op jit(solution)/shard_map/dynamic_update_slice | solution.py:224
  (142 shorter events, 63.0 us)
Async XLA Ops:
  7.2 2.0 copy-start.1
  7.2 12.5 %copy-start.8 = (s32[512,3]{0,1:T(4,128)S(1)}, s32[512,3]{0,1:T(4,128)}, u32[]{:S(2)}) copy-start(s32[512,3]{0,1:T(4,128)} %param.9) | copy-start | bytes 18436
  7.2 156.1 %all-gather.6.cloned.1.call-start = ((), (), s32[]{:S(2)}) async-start(), calls=%async_computation | async-start | bytes 4227072 | tf_op jit(solution)/shard_map/all_gather | solution.py:201
  9.2 6.8 %copy-start = (f32[3,32,32,256]{3,2,1,0:T(8,128)}, f32[3,32,32,256]{3,2,1,0:T(8,128)S(1)}, u32[]{:S(2)}) copy-start(f32[3,32,32,256]{3,2,1,0:T(8,128)S(1)} %copy.207) | copy-start | bytes 9437188
  9.9 246.5 %all-gather.8.cloned.1.call-start = ((), (), s32[]{:S(2)}) async-start(), calls=%async_computation.1 | async-start | bytes 8454144 | tf_op jit(solution)/shard_map/all_gather | solution.py:183
  10.9 17.2 %collective-permute-start = (f32[3,1,32,256]{3,2,1,0:T(8,128)S(1)}, f32[3,1,32,256]{3,2,1,0:T(8,128)S(1)}, u32[]{:S(2)}, u32[]{:S(2)}) collective-permute-start(f32[3,1,32,256]{3,2,1,0:T(8,128)S(1)} %get-tuple-element.18), channel_id=1, source_target_pairs={{0,8},{8,16},{16,24},{24,32},{32,40},{40,48},{48,56},{56,64},{64,7... | collective-permute-start | bytes 294920 | tf_op jit(solution)/shard_map/ppermute | solution.py:27
  14.7 13.5 %collective-permute-start.1 = (f32[3,1,32,256]{3,2,1,0:T(8,128)}, f32[3,1,32,256]{3,2,1,0:T(8,128)}, u32[]{:S(2)}, u32[]{:S(2)}) collective-permute-start(f32[3,1,32,256]{3,2,1,0:T(8,128)} %get-tuple-element.19), channel_id=1, source_target_pairs={{8,0},{16,8},{24,16},{32,24},{40,32},{48,40},{56,48},{64,56},{72,6... | collective-permute-start | bytes 294920 | tf_op jit(solution)/shard_map/ppermute | solution.py:29
  20.6 0.7 copy-start.11
  29.2 7.4 %collective-permute-start.2 = (f32[3,34,1,256]{3,1,2,0:T(8,128)S(1)}, f32[3,34,1,256]{3,1,2,0:T(8,128)S(1)}, u32[]{:S(2)}, u32[]{:S(2)}) collective-permute-start(f32[3,34,1,256]{3,1,2,0:T(8,128)S(1)} %get-tuple-element.16), channel_id=1, source_target_pairs={{0,2},{2,4},{4,6},{1,3},{3,5},{5,7},{8,10},{10,12},{12,14},{9,11},... | collective-permute-start | bytes 313352 | tf_op jit(solution)/shard_map/ppermute | solution.py:27
  32.7 6.8 %collective-permute-start.3 = (f32[3,34,1,256]{3,1,2,0:T(8,128)S(1)}, f32[3,34,1,256]{3,1,2,0:T(8,128)S(1)}, u32[]{:S(2)}, u32[]{:S(2)}) collective-permute-start(f32[3,34,1,256]{3,1,2,0:T(8,128)S(1)} %get-tuple-element.17), channel_id=1, source_target_pairs={{2,0},{4,2},{6,4},{3,1},{5,3},{7,5},{10,8},{12,10},{14,12},{11,9},... | collective-permute-start | bytes 313352 | tf_op jit(solution)/shard_map/ppermute | solution.py:29
  36.6 6.2 %copy-start.5 = (f32[3,34,1,256]{3,1,2,0:T(8,128)}, f32[3,34,1,256]{3,1,2,0:T(8,128)S(1)}, u32[]{:S(2)}) copy-start(f32[3,34,1,256]{3,1,2,0:T(8,128)S(1)} %collective-permute-done.2) | copy-start | bytes 313348
  39.5 3.3 copy-start.6
  49.1 11.5 %collective-permute-start.4 = (f32[3,34,34,1]{2,1,3,0:T(8,128)}, f32[3,34,34,1]{2,1,3,0:T(8,128)}, u32[]{:S(2)}, u32[]{:S(2)}) collective-permute-start(f32[3,34,34,1]{2,1,3,0:T(8,128)} %copy.144), channel_id=1, source_target_pairs={{0,1},{2,3},{4,5},{6,7},{8,9},{10,11},{12,13},{14,15},{16,17},{18,... | collective-permute-start | bytes 41624 | tf_op jit(solution)/shard_map/ppermute | solution.py:27
  51.0 6.4 %collective-permute-start.5 = (f32[3,34,34,1]{2,1,3,0:T(8,128)}, f32[3,34,34,1]{2,1,3,0:T(8,128)}, u32[]{:S(2)}, u32[]{:S(2)}) collective-permute-start(f32[3,34,34,1]{2,1,3,0:T(8,128)} %copy.145), channel_id=1, source_target_pairs={{1,0},{3,2},{5,4},{7,6},{9,8},{11,10},{13,12},{15,14},{17,16},{19,... | collective-permute-start | bytes 41624 | tf_op jit(solution)/shard_map/ppermute | solution.py:29
  68.1 307.6 %all-gather.10.cloned.1.call-start = ((), (), s32[]{:S(2)}) async-start(), calls=%async_computation.2 | async-start | bytes 3932160 | tf_op jit(solution)/shard_map/all_gather | solution.py:45
  148.0 1.9 copy-start.4
  148.0 2.0 copy-start.3
  153.3 8.2 %copy-start.9 = (s32[512]{0:T(512)S(1)}, s32[512]{0:T(512)}, u32[]{:S(2)}) copy-start(s32[512]{0:T(512)} %param.10) | copy-start | bytes 6148
  153.3 8.4 %copy-start.7 = (f32[4,16,256]{2,1,0:T(8,128)S(1)}, f32[4,16,256]{2,1,0:T(8,128)}, u32[]{:S(2)}) copy-start(f32[4,16,256]{2,1,0:T(8,128)} %param.8) | copy-start | bytes 196612
  256.4 17.5 %copy-start.2 = (f32[3,512,256]{2,0,1:T(4,128)S(1)}, f32[3,512,256]{2,0,1:T(4,128)}, u32[]{:S(2)}) copy-start(f32[3,512,256]{2,0,1:T(4,128)} %get-tuple-element.12) | copy-start | bytes 4718596
  279.4 3.8 copy-start.12
  289.1 51.0 %copy-start.10 = (pred[4]{0:T(512)(128)(4,1)S(1)}, pred[4]{0:T(512)(128)(4,1)}, u32[]{:S(2)}) copy-start(pred[4]{0:T(512)(128)(4,1)} %fusion.51) | copy-start | bytes 16
Sparse Core Ops, SparseCore 0:
  11.6 119.9 all-gather.5
  135.7 120.7 all-gather.7
  337.5 38.0 all-gather.9
where the time goes:
time: 442 us; the launch traced here: 433 us
  local copies, waits for them, and re-layouts  166 us (38%)
  waiting for transfers between devices  126 us (29%)
  other arithmetic  45.6 us (10%)
  blocking collectives  40.3 us (9%)
  between operations  21 us (5%)
  matrix products  19.6 us (4%)
  starting transfers between devices  14.7 us (3%)
    all_gather x1, waiting for transfers between devices, on_device(): lax.all_gather(cubes, GX_GY, axis=1, tiled=True)  88.9 us
    all_gather x2, blocking collectives, gather_in_order(): pieces = lax.all_gather(pieces, axes[k])  40.3 us
    reshape x6, local copies, waits for them, and re-layouts, prolong_matrix(): block.reshape(side ** 3, F * F)  38.4 us
    dynamic_update_slice x1, local copies, waits for them, and re-layouts, on_device(): coarse_out = lax.dynamic_update_slice(coarse_field, region, start)  36.5 us
    all_gather x1, waiting for transfers between devices, gather_in_order(): pieces = lax.all_gather(pieces, axes[k])  34 us
    transpose x1, other arithmetic, prolong_matrix(): jnp.einsum('sa,tb,c->abcst', tangent, tangent, high_side)  12.8 us
    dot_general x4, matrix products, collect_rows(): return jnp.einsum('sr,krw->ksw', select, piece, precision=highest)  11.6 us
    dot_general x2, local copies, waits for them, and re-layouts, on_device(): jnp.dot(picked.reshape(3 * SLOTS, CUBE), weights, precision=highest, pref...  9.83 us
  transfers between devices with their start and end apart: 9, of which 3 were waited for; matrix products, arithmetic and copies ran while one was open for 32% of the time, Pallas kernels for 0%

commit v1 on v0

v1 whole, which is shorter than its diff:
```python
import numpy as np
import jax
import jax.numpy as jnp
from jax import lax
from jax.experimental import pallas as pl
from jax.experimental.pallas import tpu as pltpu
from jax.sharding import Mesh
from jax.sharding import PartitionSpec as P

MESH = pl.DeviceIdType.MESH
VMEM = pltpu.VMEM
GX = ("gx_0", "gx_1")
GX_GY_GZ = ("gx_0", "gx_1", "gy", "gz")
B = 8
F = 16
SLOTS = 4
NXC, NZC, NYC = 4, 8, 4
HIGH = lax.Precision.HIGHEST
RATE = 0.15
PITCH = 40

T_WIN = 0
T_D = 64
T_P = 72
T_V = 136
T_OD = 168
T_OP = 169
T_OV = 177
T_ACT = 181
T_NEAR = 185
T_Q = 193
T_HERE = 197
T_SIZE = 256


def interpolation():
    t = np.zeros((F, B + 2), np.float32)
    for i in range(F):
        center = i // 2 + 1
        t[i, center] += 0.75
        t[i, center - 1 if i % 2 == 0 else center + 1] += 0.25
    return t


def constants():
    t = interpolation()
    low = np.zeros(B + 2, np.float32)
    low[0], low[1] = 0.75, 0.25
    high = low[::-1]
    side = np.zeros((3, 128, 128), np.float32)
    for c in range(3):
        for a in range(B + 2):
            for b in range(B + 2):
                side[c, a * 10 + b, c * 40 + b] += low[a]
                side[c, a * 10 + b, c * 40 + 10 + b] += high[a]
                side[c, a * 10 + b, c * 40 + 20 + a] += low[b]
                side[c, a * 10 + b, c * 40 + 30 + a] += high[b]
    along = np.zeros((SLOTS * F, 40), np.float32)
    for q in range(SLOTS):
        for i in range(F):
            for a in range(B + 2):
                x = 8 * q - 1 + a
                along[q * F + i, 32 if x < 0 else 33 if x > 31 else x] += t[i, a]
    spread = np.zeros((128, 3, F, F), np.float32)
    for c in range(3):
        for u in range(B + 2):
            spread[c * 40 + u, c, 0, :] += t[:, u]
            spread[c * 40 + 10 + u, c, F - 1, :] += t[:, u]
            spread[c * 40 + 20 + u, c, :, 0] += t[:, u]
            spread[c * 40 + 30 + u, c, :, F - 1] += t[:, u]
    face = np.zeros((128, F, F), np.float32)
    face[:100] = np.einsum("ja,lb->abjl", t, t).reshape(100, F, F)
    pair_yz = np.zeros((2, F, F, 128), np.float32)
    for h in range(2):
        for j in range(F):
            for l in range(F):
                pair_yz[h, j, l, h * 64 + (7 - j // 2) * 8 + l // 2] = 0.25
    pair_x = np.zeros((2, 48, 3, SLOTS, F), np.float32)
    for h in range(2):
        for s in range(SLOTS):
            for c in range(3):
                for r in range(4):
                    row = s * 8 + c * 4 + r if c < 2 else 32 + s * 4 + r
                    pair_x[h, row, c, s, 4 * r + 2 * h : 4 * r + 2 * h + 2] = 0.5
    return (
        side,
        along,
        spread.reshape(128, 3 * F * F),
        face.reshape(128, F * F),
        pair_yz.reshape(2, F * F, 128),
        pair_x.reshape(2, 48, 3 * SLOTS * F),
    )


def index_table(corners, grid_slot, neighbors):
    ix, iz = lax.axis_index("gx_0"), lax.axis_index("gx_1")
    iy, ik = lax.axis_index("gy"), lax.axis_index("gz")
    i32 = jnp.int32
    grids = jnp.arange(corners.shape[0], dtype=i32)
    cx, cy, cz = corners[:, 0], corners[:, 1], corners[:, 2]
    brick = (cx // 32 * NYC + cy // 32) * 2 + cz // 256
    box = cx // B % SLOTS
    place = cy % 32 * 256 + cz % 256
    match = neighbors[:, :, None] == grids[None, None, :]
    near_slot = jnp.sum(jnp.where(match, grid_slot[None, None, :] + 1, 0), axis=2) - 1

    def pick(mask, value):
        return jnp.max(jnp.where(mask, value, -1), axis=-1)

    dy, dk, dx = np.meshgrid([-1, 0, 1], [0, 1], [-1, 0, 1], indexing="ij")
    dy, dk, dx = (jnp.asarray(v.reshape(-1), i32) for v in (dy, dk, dx))
    bx = (ix * NZC + iz + dx) % 32
    by = (iy + dy) % NYC
    bk = (ik + dk) % 2
    near_brick = (bx * NYC + by) * 2 + bk
    found = jnp.maximum(pick(near_brick[:, None] == brick[None, :], place[None, :]), 0)
    win = jnp.stack([found // 256 + (by - iy) * 32, found % 256 + (bk - ik) * 256], axis=1)
    step = jnp.arange(NZC, dtype=i32)
    to_z = (iz + step) % NZC
    device = ((ix * NZC + to_z) * NYC + iy) * 2 + ik
    slot = device[:, None] * SLOTS + jnp.arange(SLOTS, dtype=i32)
    own = slot[:, :, None] == grid_slot
    slot_brick = pick(own, brick)
    slot_box = pick(own, box)
    slot_near = jnp.stack([pick(own, near_slot[:, 0]), pick(own, near_slot[:, 1])], axis=2)
    source = jnp.maximum(jnp.max(slot_brick, axis=1), 0)

    def turn(x, y):
        return (ix - x) % NXC * NYC + (iy - y) % NYC

    def lies(n):
        return n // 64, n // 8 % NZC, n // 2 % NYC

    sx, sz, sy = lies(source)
    t_d = jnp.where(sz == iz, turn(sx, sy), 0)
    near = jnp.maximum(slot_near, 0)
    px, pz, py = lies(near // SLOTS)
    sides = jnp.arange(2, dtype=i32)
    t_p = jnp.where(pz == iz, turn(px, py) * 8 + near % SLOTS * 2 + sides, 0)
    here = (brick == device[:, None])[:, None, :] & (box == jnp.arange(SLOTS, dtype=i32)[:, None])[None]
    home = pick(here, grid_slot)
    held = jnp.maximum(home, 0)
    vx, vz, vy = lies(held // SLOTS)
    t_v = jnp.where(vz == iz, turn(vx, vy) * SLOTS + held % SLOTS, 0)
    parts = [
        win.reshape(-1),
        jnp.zeros(T_D - 36, i32),
        t_d,
        t_p.reshape(-1),
        t_v.reshape(-1),
        (iz - sz[:1]) % NZC,
        ((iz - pz[0]) % NZC).reshape(-1),
        (iz - vz[0]) % NZC,
        (slot_brick[0] >= 0).astype(i32),
        (slot_near[0] >= 0).astype(i32).reshape(-1),
        jnp.maximum(slot_box[0], 0),
        (jnp.max(home[0]) >= 0).astype(i32)[None],
        jnp.zeros(T_SIZE - T_HERE - 1, i32),
    ]
    return jnp.concatenate(parts)


def window_kernel(tab, coarse, own, other, beside, brick, sems):
    copies = [
        pltpu.make_async_copy(
            coarse.at[:, :, :, pl.ds(h * 128, 128)], brick.at[h, :, :, pl.ds(0, 32), :], sems.at[h]
        )
        for h in range(2)
    ]
    for copy in copies:
        copy.start()
    flat = brick.reshape(2 * 3 * 32 * PITCH, 128)
    lane = lax.broadcasted_iota(jnp.int32, (1, 128), 1)
    sub = lax.broadcasted_iota(jnp.int32, (8, 128), 0)

    class Window:
        def __init__(self, dy, core, dx):
            at = T_WIN + 2 * ((dy + 1) * 6 + core * 3 + dx + 1)
            self.y, self.z = tab[at], tab[at + 1]
            z = self.z & 255
            self.half, shift = z >> 7, z & 127
            self.first = (shift - 1) & 127
            self.cross = ((shift == 0) & (lane == 127)) | ((shift == 120) & (lane == 0))

        def row(self, c, yy, base, x=None):
            y = self.y - 1 + yy
            inside = (y >= 0) & (y < 32)
            y = jnp.clip(y, 0, 31)

            def take(half):
                start = half * (3 * 32 * PITCH) + c * (32 * PITCH) + y
                if x is None:
                    return flat[pl.ds(start, 32, stride=PITCH), :]
                return flat[pl.ds(start + x * PITCH, 1), :]

            line = jnp.where(self.cross, take(1 - self.half), take(self.half))
            line = pltpu.roll(line, (base - self.first) & 127, 1)
            t = lane - base
            z = self.z - 1 + t
            keep = (t >= 0) & (t < 10) & (z >= 0) & (z < 256) & inside
            return jnp.where(keep, line, 0.0)

    for copy in copies:
        copy.wait()
    for core, out in ((0, own), (1, other)):
        mid, left, right = (Window(0, core, dx) for dx in (0, -1, 1))
        for c in range(3):
            body = jnp.zeros((32, 128), jnp.float32)
            low = jnp.zeros((1, 128), jnp.float32)
            high = jnp.zeros((1, 128), jnp.float32)
            for yy in range(10):
                body += mid.row(c, yy, yy * 10)
                low += right.row(c, yy, yy * 10, 31)
                high += left.row(c, yy, yy * 10, 0)
            out[c, 0:32, :] = body
            out[c, 32:40, :] = jnp.where(sub == 0, low, jnp.where(sub == 1, high, 0.0))
    for n, (dy, core) in enumerate(((-1, 0), (-1, 1), (1, 0), (1, 1))):
        yy = 9 if dy < 0 else 0
        mid, left, right = (Window(dy, core, dx) for dx in (0, -1, 1))
        body = jnp.zeros((32, 128), jnp.float32)
        low = jnp.zeros((1, 128), jnp.float32)
        high = jnp.zeros((1, 128), jnp.float32)
        for c in range(3):
            body += mid.row(c, yy, c * 10)
            low += right.row(c, yy, c * 10, 31)
            high += left.row(c, yy, c * 10, 0)
        beside[n, 0:32, :] = body
        beside[n, 32:40, :] = jnp.where(sub == 0, low, jnp.where(sub == 1, high, 0.0))


def dot(a, b):
    return jnp.dot(a, b, precision=HIGH, preferred_element_type=jnp.float32)


def exchange_kernel(
    tab, fine, visc, own, other, beside, side, along, spread, face, pair_yz, pair_x,
    fine_out, boxes,
    planes, near_z, near_y, edge, edges, ghost, planes_in, ghost_in, planes_to, ghost_to,
    planes_at, ghost_at, pull, adv, means, means_in, means_to, means_at,
    y_send, y_recv, x_send, x_recv, p_send, p_recv, g_send, g_recv, m_send, m_recv,
    pz_send, pz_recv, gz_send, gz_recv, mz_send, mz_recv,
):
    ix, iz = lax.axis_index("gx_0"), lax.axis_index("gx_1")
    iy, ik = lax.axis_index("gy"), lax.axis_index("gz")

    def device(x, z, y, k):
        return {"gx_0": x, "gx_1": z, "gy": y, "gz": k}

    plane_peers = [
        (n, device((ix + n // NYC) % NXC, iz, (iy + n % NYC) % NYC, ik)) for n in range(1, NXC * NYC)
    ]
    line_peers = [(n, device(ix, (iz + n) % NZC, iy, ik)) for n in range(1, NZC)]
    chain = ix * NZC + iz
    up, down = (chain + 1) % 32, (chain + 31) % 32
    x_peers = [(0, device(up // NZC, up % NZC, iy, ik)), (1, device(down // NZC, down % NZC, iy, ik))]
    y_peers = [
        (n, device(ix, iz, (iy + dy) % NYC, (ik + dk) % 2))
        for n, (dy, dk) in enumerate(((3, 0), (3, 1), (1, 0), (1, 1)))
    ]
    partner = device(ix, iz, iy, 1 - ik)

    def send(src, dst, send_sem, recv_sem, to):
        copy = pltpu.make_async_remote_copy(
            src_ref=src, dst_ref=dst, send_sem=send_sem, recv_sem=recv_sem, device_id=to, device_id_type=MESH
        )
        copy.start()
        return copy

    barrier = pltpu.get_barrier_semaphore()
    greeted = plane_peers + line_peers + x_peers + [y_peers[1], y_peers[3], (0, partner)]
    for _, to in greeted:
        pl.semaphore_signal(barrier, inc=1, device_id=to, device_id_type=MESH)

    for s in range(SLOTS):
        for d in range(2):
            x = F - 1 if d == 0 else 0
            rows = [fine[c, s, x : x + 1, h * 128 : h * 128 + 128] for c in range(3) for h in range(2)]
            tile = jnp.concatenate(rows + [jnp.zeros((2, 128), jnp.float32)], axis=0)
            planes[s * 2 + d] = tile
            planes_in[0, s * 2 + d] = tile
    pl.semaphore_wait(barrier, len(greeted))
    sent = []
    first = [send(other, near_z, y_send.at[4], y_recv.at[4], partner)]
    first += [send(beside.at[n], near_y.at[n], y_send.at[n], y_recv.at[n], to) for n, to in y_peers]
    p_copies = [send(planes, planes_in.at[n], p_send.at[n], p_recv.at[n], to) for n, to in plane_peers]
    for copy in first:
        copy.wait_recv()
    lane = lax.broadcasted_iota(jnp.int32, (1, 128), 1)
    sub = lax.broadcasted_iota(jnp.int32, (8, 128), 0)
    upper = near_y[0] + near_y[1]
    lower = near_y[2] + near_y[3]
    window = []
    for c in range(3):
        cells = own[c] + near_z[c]
        cells += jnp.where((lane >= 90) & (lane < 100), pltpu.roll(upper, 90 - 10 * c, 1), 0.0)
        cells += jnp.where(lane < 10, pltpu.roll(lower, (128 - 10 * c) % 128, 1), 0.0)
        window.append(cells)
        edge[c] = cells[32:40]
    x_copies = [send(edge, edges.at[n], x_send.at[n], x_recv.at[n], to) for n, to in x_peers]

    for copy in p_copies:
        copy.wait_recv()
    pz_copies = []
    for n in range(NZC):
        for j in range(2 * SLOTS):
            at = tab[T_P + n * 8 + j]
            tile = planes_in[at // 8, at % 8]
            if n:
                planes_to[n, j] = tile
            else:
                planes_at[0, j] = tile
        if n:
            pz_copies.append(
                send(planes_to.at[n], planes_at.at[n], pz_send.at[n], pz_recv.at[n], line_peers[n - 1][1])
            )

    for copy in x_copies:
        copy.wait_recv()
    total = jnp.zeros((40, 128), jnp.float32)
    ends = jnp.zeros((8, 128), jnp.float32)
    for c in range(3):
        from_low = jnp.where(chain > 0, edges[0, c], 0.0)
        from_high = jnp.where(chain < 31, edges[1, c], 0.0)
        tile = jnp.where(sub == 0, from_low, jnp.where(sub == 1, from_high, 0.0))
        body = window[c][0:32]
        total += dot(jnp.concatenate([body, tile], axis=0), side[c])
        low = 0.75 * tile[0:1] + 0.25 * body[0:1]
        high = 0.75 * tile[1:2] + 0.25 * body[31:32]
        ends += jnp.where(sub == 2 + 2 * c, low, jnp.where(sub == 3 + 2 * c, high, 0.0))
    total = jnp.concatenate([total[0:32], jnp.where(sub < 2, total[32:40], ends)], axis=0)
    ghost[...] = total
    ghost_in[0] = total
    g_copies = [send(ghost, ghost_in.at[n], g_send.at[n], g_recv.at[n], to) for n, to in plane_peers]
    for copy in g_copies:
        copy.wait_recv()
    gz_copies = []
    for n in range(NZC):
        block = ghost_in[tab[T_D + n]]
        if n:
            ghost_to[n] = block
            gz_copies.append(
                send(ghost_to.at[n], ghost_at.at[n], gz_send.at[n], gz_recv.at[n], line_peers[n - 1][1])
            )
        else:
            ghost_at[0] = block
    for copy in pz_copies + gz_copies:
        copy.wait_recv()

    block = ghost_at[tab[T_OD]]
    lines = dot(along[...], block)
    pulled = dot(lines, spread[...])
    for q in range(SLOTS):
        pull[q] = pulled[q * F : q * F + F]
    faces = dot(block[32:40], face[...])

    lane = lax.broadcasted_iota(jnp.int32, (F, F * F), 1)
    row = lax.broadcasted_iota(jnp.int32, (F, F * F), 0)
    for s in range(SLOTS):
        rate = RATE * visc[s]
        ghosts = pull[tab[T_Q + s]]
        active = tab[T_ACT + s] > 0
        tiles = [planes_at[tab[T_OP + s * 2 + d], s * 2 + d] for d in range(2)]
        near = [tab[T_NEAR + s * 2 + d] > 0 for d in range(2)]
        for c in range(3):
            cells = fine[c, s]
            ends = [
                jnp.where(
                    near[d],
                    jnp.concatenate([tiles[d][2 * c : 2 * c + 1], tiles[d][2 * c + 1 : 2 * c + 2]], axis=1),
                    faces[2 + 2 * c + d : 3 + 2 * c + d],
                )
                for d in range(2)
            ]
            around = ghosts[:, c * F * F : (c + 1) * F * F] - 6.0 * cells
            around += jnp.where(row == 0, ends[0], pltpu.roll(cells, 1, 0))
            around += jnp.where(row == F - 1, ends[1], pltpu.roll(cells, F - 1, 0))
            around += jnp.where(lane < F, 0.0, pltpu.roll(cells, F, 1))
            around += jnp.where(lane >= F * F - F, 0.0, pltpu.roll(cells, F * F - F, 1))
            around += jnp.where(lane % F == 0, 0.0, pltpu.roll(cells, 1, 1))
            around += jnp.where(lane % F == F - 1, 0.0, pltpu.roll(cells, F * F - 1, 1))
            moved = cells + rate * around
            fine_out[c, s] = jnp.where(active, moved, 0.0)
            adv[(c * SLOTS + s) * F : (c * SLOTS + s + 1) * F, :] = moved

    cells = adv[...]
    mean = dot(pair_x[0], dot(cells, pair_yz[0])) + dot(pair_x[1], dot(cells, pair_yz[1]))
    for j in range(6):
        means[j] = mean[j * 8 : j * 8 + 8]
        means_in[0, j] = mean[j * 8 : j * 8 + 8]
    m_copies = [send(means, means_in.at[n], m_send.at[n], m_recv.at[n], to) for n, to in plane_peers]
    for copy in m_copies:
        copy.wait_recv()

    def third(tiles_of, q_low):
        halves = []
        for h in range(2):
            tile, odd = tiles_of(q_low + h)
            flip = (odd == 1) if h == 0 else (odd == 0)
            halves.append(jnp.where(flip, pltpu.roll(tile, 4, 0), tile))
        return jnp.where(sub < 4, halves[0], halves[1])

    mz_copies = []
    for n in range(NZC):
        out = means_to.at[n] if n else means_at.at[0]
        for q in range(SLOTS):
            at = tab[T_V + n * 4 + q]
            out[q] = means_in[at // 4, at % 4]

        def tiles_of(q, n=n):
            at = tab[T_V + n * 4 + q]
            return means_in[at // 4, 4 + at % 4 // 2], at % 2

        for h in range(2):
            out[4 + h] = third(tiles_of, 2 * h)
        if n:
            mz_copies.append(
                send(means_to.at[n], means_at.at[n], mz_send.at[n], mz_recv.at[n], line_peers[n - 1][1])
            )
    for copy in mz_copies:
        copy.wait_recv()
    for q in range(SLOTS):
        boxes[q] = means_at[tab[T_OV + q], q]
    for h in range(2):
        boxes[4 + h] = jnp.where(
            sub < 4, means_at[tab[T_OV + 2 * h], 4 + h], means_at[tab[T_OV + 2 * h + 1], 4 + h]
        )
    for copies in (first, p_copies, x_copies, pz_copies, g_copies, gz_copies, m_copies, mz_copies):
        for copy in copies:
            copy.wait_send()


def place_kernel(tab, boxes, coarse, out, brick, in_sems, out_sems):
    reads = [pltpu.make_async_copy(coarse.at[c], brick.at[c], in_sems.at[c]) for c in range(3)]
    for copy in reads:
        copy.start()
    at = T_WIN + 2 * (6 + 1)
    y, z = tab[at], tab[at + 1]
    shift = z & 127
    here = tab[T_HERE] > 0
    lane = lax.broadcasted_iota(jnp.int32, (8, 128), 1)
    keep = (lane >= shift) & (lane < shift + 8) & here
    y = pl.multiple_of(y, 8)
    z = pl.multiple_of(z - shift, 128)
    writes = []
    for c in range(3):
        reads[c].wait()
        for q in range(SLOTS):
            for a in range(B):
                r = a // 2
                tile, r = (q, c * 4 + r) if c < 2 else (4 + q // 2, q % 2 * 4 + r)
                line = jnp.broadcast_to(boxes[tile, r : r + 1, :], (8, 128))
                line = pltpu.roll(pltpu.roll(line, 72 - 64 * (a % 2), 1, stride=8, stride_axis=0), shift, 1)
                spot = (c, q * B + a, pl.ds(y, 8), pl.ds(z, 128))
                brick[spot] = jnp.where(keep, line, brick[spot])
        copy = pltpu.make_async_copy(brick.at[c], out.at[c], out_sems.at[c])
        copy.start()
        writes.append(copy)
    for copy in writes:
        copy.wait()


def spec(space):
    return pl.BlockSpec(memory_space=space)


def on_device(coarse, fine, visc, corners, grid_slot, neighbors):
    f32 = jnp.float32
    tab = index_table(corners, grid_slot, neighbors)
    own, other, beside = pl.pallas_call(
        window_kernel,
        out_shape=(
            jax.ShapeDtypeStruct((3, 40, 128), f32),
            jax.ShapeDtypeStruct((3, 40, 128), f32),
            jax.ShapeDtypeStruct((4, 40, 128), f32),
        ),
        in_specs=[spec(pltpu.SMEM), spec(pl.ANY)],
        out_specs=(spec(VMEM),) * 3,
        scratch_shapes=[VMEM((2, 3, 32, PITCH, 128), f32), pltpu.SemaphoreType.DMA((2,))],
        name="windows",
    )(tab, coarse)
    dma = pltpu.SemaphoreType.DMA
    n_plane, n_line = NXC * NYC, NZC
    fine_out, boxes = pl.pallas_call(
        exchange_kernel,
        out_shape=(jax.ShapeDtypeStruct(fine.shape, f32), jax.ShapeDtypeStruct((6, 8, 128), f32)),
        in_specs=[spec(pltpu.SMEM)] + [spec(VMEM)] * 11,
        out_specs=(spec(VMEM),) * 2,
        scratch_shapes=[
            VMEM((8, 8, 128), f32),
            VMEM((3, 40, 128), f32),
            VMEM((4, 40, 128), f32),
            VMEM((3, 8, 128), f32),
            VMEM((2, 3, 8, 128), f32),
            VMEM((40, 128), f32),
            VMEM((n_plane, 8, 8, 128), f32),
            VMEM((n_plane, 40, 128), f32),
            VMEM((n_line, 8, 8, 128), f32),
            VMEM((n_line, 40, 128), f32),
            VMEM((n_line, 8, 8, 128), f32),
            VMEM((n_line, 40, 128), f32),
            VMEM((SLOTS, F, 3 * F * F), f32),
            VMEM((3 * SLOTS * F, F * F), f32),
            VMEM((6, 8, 128), f32),
            VMEM((n_plane, 6, 8, 128), f32),
            VMEM((n_line, 6, 8, 128), f32),
            VMEM((n_line, 6, 8, 128), f32),
        ]
        + [dma((5,)), dma((5,)), dma((2,)), dma((2,))]
        + [dma((n_plane,))] * 6
        + [dma((n_line,))] * 6,
        compiler_params=pltpu.CompilerParams(collective_id=1, has_side_effects=True),
        name="exchange",
    )(tab, fine, visc, own, other, beside, *(jnp.asarray(v) for v in constants()))
    coarse_out = pl.pallas_call(
        place_kernel,
        out_shape=jax.ShapeDtypeStruct(coarse.shape, f32),
        in_specs=[spec(pltpu.SMEM), spec(VMEM), spec(pl.ANY)],
        out_specs=spec(pl.ANY),
        scratch_shapes=[VMEM(coarse.shape, f32), dma((3,)), dma((3,))],
        name="place",
    )(tab, boxes, coarse)
    return fine_out, coarse_out


def solution(mesh):
    split = Mesh(
        mesh.devices.reshape(NXC, NZC, mesh.shape["gy"], mesh.shape["gz"]), ("gx_0", "gx_1", "gy", "gz")
    )
    in_specs = (
        P(None, GX, "gy", "gz"),
        P(None, GX_GY_GZ, None, None),
        P(GX_GY_GZ, None, None),
        P(),
        P(),
        P(),
    )
    out_specs = (P(None, GX_GY_GZ, None, None), P(None, GX, "gy", "gz"))
    return jax.shard_map(on_device, mesh=split, in_specs=in_specs, out_specs=out_specs, check_vma=False)
```

time: 442 us -> 71.4 us (0.16)
  the two profiles are of different devices: /device:TPU:8 before, /device:TPU:16 now
where the time goes in v1:
time: 71.4 us
  Pallas kernels  60.3 us (84%)
  other arithmetic  5.3 us (7%)
  local copies, waits for them, and re-layouts  4.27 us (6%)
  between operations  1.52 us (2%)
    pallas_call x1, Pallas kernels, on_device(): pl.pallas_call(exchange_kernel, out_shape=(jax.ShapeDtypeStruct(fine.shap...  52.2 us
    pallas_call x1, Pallas kernels, on_device(): pl.pallas_call(window_kernel, out_shape=(jax.ShapeDtypeStruct((3, 40, 128...  4.18 us
    pallas_call x1, Pallas kernels, on_device(): pl.pallas_call(place_kernel, out_shape=jax.ShapeDtypeStruct(coarse.shape,...  3.93 us
    reduce_max x2, other arithmetic, pick(): return jnp.max(jnp.where(mask, value, -1), axis=-1)  1.46 us

profile of v1, /device:TPU:16, one launch (start us, length us, event | category | flops | bytes accessed | tf_op | source)
XLA Modules:
  0.0 71.4 jit_solution(2903584060941301713)
XLA Ops:
  0.7 0.7 fusion.33
  1.4 0.7 broadcast_add_fusion.1
  2.1 1.1 %select_reduce_fusion = s32[512,2]{0,1:T(2,128)S(1)} fusion(s32[512]{0:T(512)S(1)} %broadcast_add_fusion.1, s32[512,2]{0,1:T(2,128)} %param.20), kind=kLoop, calls=%fused_computation | loop fusion | flops 1571840 | bytes 10240 | tf_op jit(solution)/shard_map/reduce_sum | solution.py:105
  3.2 0.8 %fusion.65 = (s32[512,1]{0,1:T(1,128)S(1)}, s32[512,1]{0,1:T(1,128)S(1)}, s32[512,1]{0,1:T(1,128)S(1)}) fusion(s32[512,3]{0,1:T(4,128)} %param.18), kind=kLoop, calls=%fused_computation.226 | loop fusion | bytes 12288 | tf_op jit(solution)/shard_map/slice | solution.py:100
  4.1 0.2 select_reduce_fusion.2
  4.4 1.3 %fusion.4 = (s32[8,4]{0,1:T(4,128)S(1)}, s32[8,4]{0,1:T(4,128)S(1)}, s32[8,4]{0,1:T(4,128)S(1)}, s32[8]{0:T(128)S(1)}, s32[8,4]{0,1:T(4,128)S(1)}, /*index=5*/s32[8,4]{0,1:T(4,128)S(1)}) fusion(s32[512]{0:T(512)S(1)} %get-tuple-element.42, s32[512]{0:T(512)} %param.19, s32[8,4]{0,1:T(4,128)S(1)} %iota_add_fusion, s32[512]{0:T(512)S(1)} %bitcast.17, ...), kind=kLoop, calls=%fused_computation.10 | loop fusion | flops 212824 | bytes 17184 | tf_op jit(solution)/shard_map/reduce_max | solution.py:108
  5.7 0.1 maximum_reduce_fusion
  5.8 0.7 convert_reduce_fusion
  7.1 0.1 copy.51
  7.3 0.1 copy.59
  7.4 0.1 reshape.306
  7.5 0.1 copy.52
  7.6 0.1 ne.432
  7.8 0.1 subtract_reduce_fusion
  7.9 0.1 copy.55
  8.0 0.1 ne.447
  8.2 0.1 rem.721
  8.3 0.1 div.190
  8.5 0.1 copy.49
  8.6 0.1 reshape.304
  8.7 0.1 add.397
  8.9 0.1 copy.58
  9.0 0.1 sub.184
  9.1 0.1 copy.53
  9.3 0.1 rem.667
  9.4 0.1 copy.54
  9.5 0.1 div.172
  9.7 0.7 concatenate.3.tab
  10.4 4.2 %windows.1 = (f32[3,40,128]{2,1,0:T(8,128)}, f32[3,40,128]{2,1,0:T(8,128)}, f32[4,40,128]{2,1,0:T(8,128)}) custom-call(s32[256]{0:T(256)} %concatenate.3.tab, f32[3,32,32,256]{3,2,1,0:T(8,128)} %coarse.3), custom_call_target="tpu_custom_call" | custom-call | tf_op jit(solution)/shard_map/windows/pallas_call | solution.py:469
  14.6 52.2 %exchange.1 = (f32[3,4,16,256]{3,2,1,0:T(8,128)}, f32[6,8,128]{2,1,0:T(8,128)}) custom-call(s32[256]{0:T(256)} %concatenate.3.tab, f32[3,4,16,256]{3,2,1,0:T(8,128)} %fine.1, f32[4,16,256]{2,1,0:T(8,128)} %visc.1, f32[3,40,128]{2,1,0:T(8,128)} %get-tuple-element.7.own, f32[3,40,128]{2,1,0:T(8,128)} %get-tuple-element.8.other, ...), custom_call_target="tpu_custom_call" | custom-call | tf_op jit(solution)/shard_map/exchange/pallas_call | solution.py:483
  66.7 3.9 %place.1 = f32[3,32,32,256]{3,2,1,0:T(8,128)} custom-call(s32[256]{0:T(256)} %concatenate.3.tab, f32[6,8,128]{2,1,0:T(8,128)} %get-tuple-element.11.boxes, f32[3,32,32,256]{3,2,1,0:T(8,128)} %coarse.3), custom_call_target="tpu_custom_call" | custom-call | tf_op jit(solution)/shard_map/place/pallas_call | solution.py:514
  70.7 0.7 copy.61
  (27 shorter events, 0.7 us)
Async XLA Ops:
  66.7 3.9 %copy-start = (f32[3,4,16,256]{3,2,1,0:T(8,128)S(1)}, f32[3,4,16,256]{3,2,1,0:T(8,128)}, u32[]{:S(2)}) copy-start(f32[3,4,16,256]{3,2,1,0:T(8,128)} %get-tuple-element.50) | copy-start | bytes 589828

commit v2 on v1

v2 whole, which is shorter than its diff:
```python
import numpy as np
import jax
import jax.numpy as jnp
from jax import lax
from jax.experimental import pallas as pl
from jax.experimental.pallas import tpu as pltpu
from jax.sharding import Mesh
from jax.sharding import PartitionSpec as P

MESH = pl.DeviceIdType.MESH
VMEM = pltpu.VMEM
GX = ("gx_0", "gx_1")
GX_GY_GZ = ("gx_0", "gx_1", "gy", "gz")
B = 8
F = 16
SLOTS = 4
NXC, NZC, NYC = 4, 8, 4
RATE = 0.15
PITCH = 40

T_PLANE = 0
T_GHOST = 1
T_MEAN = 2
T_PLANE_AT = 3
T_GHOST_AT = 4
T_MEAN_AT = 5
T_NEAR = 6
T_ACTIVE = 7
T_BOX = 8
T_HERE = 9
T_Y = 10
T_Z = 11
T_ROWS = 16
LINE, PLANE = NZC, NXC * NYC


def interpolation():
    t = np.zeros((F, B + 2), np.float32)
    for i in range(F):
        center = i // 2 + 1
        t[i, center] += 0.75
        t[i, center - 1 if i % 2 == 0 else center + 1] += 0.25
    return t


def constants():
    t = interpolation()
    low = np.zeros(B + 2, np.float32)
    low[0], low[1] = 0.75, 0.25
    high = low[::-1]
    side = np.zeros((3, 128, 128), np.float32)
    for c in range(3):
        for a in range(B + 2):
            for b in range(B + 2):
                side[c, a * 10 + b, c * 40 + b] += low[a]
                side[c, a * 10 + b, c * 40 + 10 + b] += high[a]
                side[c, a * 10 + b, c * 40 + 20 + a] += low[b]
                side[c, a * 10 + b, c * 40 + 30 + a] += high[b]
    along = np.zeros((SLOTS * F, 40), np.float32)
    for q in range(SLOTS):
        for i in range(F):
            for a in range(B + 2):
                x = 8 * q - 1 + a
                along[q * F + i, 32 if x < 0 else 33 if x > 31 else x] += t[i, a]
    spread = np.zeros((128, 3, F, F), np.float32)
    for c in range(3):
        for u in range(B + 2):
            spread[c * 40 + u, c, 0, :] += t[:, u]
            spread[c * 40 + 10 + u, c, F - 1, :] += t[:, u]
            spread[c * 40 + 20 + u, c, :, 0] += t[:, u]
            spread[c * 40 + 30 + u, c, :, F - 1] += t[:, u]
    face = np.zeros((128, F, F), np.float32)
    face[:100] = np.einsum("ja,lb->abjl", t, t).reshape(100, F, F)
    pair_yz = np.zeros((F, F, 256), np.float32)
    for h in range(2):
        for j in range(F):
            for l in range(F):
                pair_yz[j, l, h * 128 + h * 64 + (7 - j // 2) * 8 + l // 2] = 0.25
    pair_x = np.zeros((2, 2, SLOTS, 8, 3, SLOTS, F), np.float32)
    for part in range(2):
        for h in range(2):
            for s in range(SLOTS):
                for c in range(3):
                    for r in range(2):
                        i = 2 * (2 * (2 * part + r) + h)
                        pair_x[h, part, s, 2 * c + r, c, s, i : i + 2] = 0.5
    return (
        side,
        along,
        spread.reshape(128, 3 * F * F),
        face.reshape(128, F * F),
        pair_yz.reshape(F * F, 256),
        pair_x.reshape(2, 2 * SLOTS * 8, 3 * SLOTS * F),
    )


def index_table(corners, grid_slot, near, ix, iz, iy, ik):
    i32 = jnp.int32
    gs = grid_slot[...]
    cx, cy, cz = corners[0:1], corners[1:2], corners[2:3]
    brick = ((cx >> 5) * NYC + (cy >> 5)) * 2 + (cz >> 8)
    box = (cx >> 3) & 3
    place = (cy & 31) * 256 + (cz & 255)
    total = gs.shape[1]
    grids = lax.broadcasted_iota(i32, (1, total), 1)

    def pick(mask, value):
        return jnp.max(jnp.where(mask, value, -1), axis=1, keepdims=True)

    def lies(n):
        return n >> 6, (n >> 3) & 7, (n >> 1) & 3

    def turn(x, y):
        return ((ix - x) & 3) * NYC + ((iy - y) & 3)

    def block(count, device, side, gather, at):
        n = lax.broadcasted_iota(i32, (count, 1), 0)
        slot = device(n >> 2) * SLOTS + (n & 3)
        own = gs == slot
        beside = pick(own, near[side : side + 1])
        near_slot = jnp.maximum(pick(grids == beside, gs), 0)
        source = jnp.maximum(pick((gs >> 2) == (slot >> 2), brick), 0)
        home = pick(brick * SLOTS + box == slot, gs)
        held = jnp.maximum(home, 0)
        mine = pick(own, box)
        return (
            gather(near_slot >> 2) * SLOTS + (near_slot & 3),
            gather(source),
            gather(held >> 2) * SLOTS + (held & 3),
            at(near_slot >> 2),
            at(source),
            at(held >> 2),
            (beside >= 0).astype(i32),
            (mine >= 0).astype(i32),
            jnp.maximum(mine, 0),
            (home >= 0).astype(i32),
        )

    def plane_gather(d):
        x, z, y = lies(d)
        return jnp.where(z == iz, turn(x, y), 0)

    def line_gather(d):
        x, z, y = lies(d)
        return jnp.where((x == ix) & (y == iy), (iz - z) & 7, 0)

    def line_at(d):
        return (iz - lies(d)[1]) & 7

    def plane_at(d):
        x, _, y = lies(d)
        return turn(x, y)

    along = block(
        LINE * SLOTS,
        lambda o: ((ix * NZC + ((iz + o) & 7)) * NYC + iy) * 2 + ik,
        0, plane_gather, line_at,
    )
    across = block(
        PLANE * SLOTS,
        lambda o: ((((ix + (o >> 2)) & 3) * NZC + iz) * NYC + ((iy + o) & 3)) * 2 + ik,
        1, line_gather, plane_at,
    )
    n = lax.broadcasted_iota(i32, (24, 1), 0)
    x = (ix * NZC + iz + (n & 3) - 1) & 31
    y = (iy + (n >> 3) - 1) & 3
    k = (ik + (n >> 2)) & 1
    found = jnp.maximum(pick((x * NYC + y) * 2 + k == brick, place), 0)
    lane = lax.broadcasted_iota(i32, (1, 128), 1)
    rest = jnp.zeros((128 - 24, 1), i32)
    columns = [jnp.concatenate([a, b, jnp.zeros((32, 1), i32)], axis=0) for a, b in zip(along, across)]
    columns.append(jnp.concatenate([(found >> 8) + (y - iy) * 32, rest], axis=0))
    columns.append(jnp.concatenate([(found & 255) + (k - ik) * 256, rest], axis=0))
    table = jnp.zeros((128, 128), i32)
    for j, column in enumerate(columns):
        table = jnp.where(lane == j, column, table)
    return table.T[0:T_ROWS]


class Window:
    def __init__(self, tab, flat, dy, core, dx):
        at = (dy + 1) * 8 + core * 4 + dx + 1
        self.flat, self.y, self.z = flat, tab[T_Y, at], tab[T_Z, at]
        z = self.z & 255
        self.half, shift = z >> 7, z & 127
        self.first = (shift - 1) & 127
        self.lane = lax.broadcasted_iota(jnp.int32, (1, 128), 1)
        self.cross = ((shift == 0) & (self.lane == 127)) | ((shift == 120) & (self.lane == 0))

    def row(self, c, yy, base, x=None):
        y = self.y - 1 + yy
        inside = (y >= 0) & (y < 32)
        y = jnp.clip(y, 0, 31)

        def take(half):
            start = half * (3 * 32 * PITCH) + c * (32 * PITCH) + y
            if x is None:
                return self.flat[pl.ds(start, 32, stride=PITCH), :]
            return self.flat[pl.ds(start + x * PITCH, 1), :]

        line = jnp.where(self.cross, take(1 - self.half), take(self.half))
        line = pltpu.roll(line, (base - self.first) & 127, 1)
        t = self.lane - base
        z = self.z - 1 + t
        keep = (t >= 0) & (t < 10) & (z >= 0) & (z < 256) & inside
        return jnp.where(keep, line, 0.0)


def parts_of(a):
    first = a.astype(jnp.bfloat16)
    a = a - first.astype(jnp.float32)
    second = a.astype(jnp.bfloat16)
    return first, second, (a - second.astype(jnp.float32)).astype(jnp.bfloat16)


def dot_right(a, weights):
    return sum(jnp.dot(p, weights, preferred_element_type=jnp.float32) for p in parts_of(a))


def dot_left(weights, a):
    return sum(jnp.dot(weights, p, preferred_element_type=jnp.float32) for p in parts_of(a))


def exchange_kernel(
    corners_in, grid_slot_in, near_in, coarse, fine_in, visc_in, side_in, along_in, spread_in, face_in,
    pair_yz_in, pair_x_in,
    result,
    corners, grid_slot, near, fine, visc, side, along, spread, face, pair_yz, pair_x,
    table, tab, brick, own, other, beside, near_z, near_y, edge, edges, pull, adv,
    planes_a, planes_b, ghost_a, ghost_b, means_a, means_b,
    planes_a_in, planes_b_in, ghost_a_in, ghost_b_in, means_a_in, means_b_in,
    planes_a_to, planes_b_to, ghost_a_to, ghost_b_to, means_a_to, means_b_to,
    planes_a_at, planes_b_at, ghost_a_at, ghost_b_at, means_a_at, means_b_at,
    input_sems, local, y_send, y_recv, x_send, x_recv, gather_send, gather_recv, pass_send, pass_recv,
):
    ix, iz = lax.axis_index("gx_0"), lax.axis_index("gx_1")
    iy, ik = lax.axis_index("gy"), lax.axis_index("gz")

    def device(x, z, y, k):
        return {"gx_0": x, "gx_1": z, "gy": y, "gz": k}

    def far(n, count):
        return min(n, count - n)

    plane_peers = [
        (n, device((ix + n // NYC) % NXC, iz, (iy + n % NYC) % NYC, ik))
        for n in sorted(range(1, PLANE), key=lambda n: -far(n // NYC, NXC) - far(n % NYC, NYC))
    ]
    line_peers = [
        (n, device(ix, (iz + n) % NZC, iy, ik)) for n in sorted(range(1, LINE), key=lambda n: -far(n, NZC))
    ]
    chain = ix * NZC + iz
    up, down = (chain + 1) % 32, (chain + 31) % 32
    x_peers = [(0, device(up // NZC, up % NZC, iy, ik)), (1, device(down // NZC, down % NZC, iy, ik))]
    beside_of = ((-1, 0), (-1, 1), (1, 0), (1, 1))
    y_peers = [
        (n, device(ix, iz, (iy + dy) % NYC, (ik + dk) % 2)) for n, (dy, dk) in enumerate(beside_of)
    ]
    partner = device(ix, iz, iy, 1 - ik)
    started = []

    def send(src, dst, send_sem, recv_sem, to):
        copy = pltpu.make_async_remote_copy(
            src_ref=src, dst_ref=dst, send_sem=send_sem, recv_sem=recv_sem, device_id=to, device_id_type=MESH
        )
        copy.start()
        started.append(copy)
        return copy

    def gather(src, dst, peers, item):
        return [
            send(src, dst.at[n], gather_send.at[item, n], gather_recv.at[item, n], to) for n, to in peers
        ]

    def passed(take, to_ref, at_ref, peers, item):
        copies = []
        for n, to in peers:
            take(n, to_ref.at[n])
            copies.append(send(to_ref.at[n], at_ref.at[n], pass_send.at[item, n], pass_recv.at[item, n], to))
        take(0, at_ref.at[0])
        return copies

    def arrive(copies):
        for copy in copies:
            copy.wait_recv()

    loads = [
        pltpu.make_async_copy(
            coarse.at[:, :, :, pl.ds(h * 128, 128)], brick.at[h, :, :, pl.ds(0, 32), :], local.at[h]
        )
        for h in range(2)
    ]
    inputs = [
        pltpu.make_async_copy(src, dst, input_sems.at[n])
        for n, (src, dst) in enumerate(
            (
                (corners_in, corners), (grid_slot_in, grid_slot), (near_in, near), (fine_in, fine),
                (visc_in, visc), (side_in, side), (along_in, along), (spread_in, spread),
                (face_in, face), (pair_yz_in, pair_yz), (pair_x_in, pair_x),
            )
        )
    ]
    for copy in inputs[:4] + loads + inputs[4:]:
        copy.start()
    barrier = pltpu.get_barrier_semaphore()
    greeted = plane_peers + line_peers + x_peers + [y_peers[1], y_peers[3], (0, partner)]
    for _, to in greeted:
        pl.semaphore_signal(barrier, inc=1, device_id=to, device_id_type=MESH)

    for copy in inputs[:3]:
        copy.wait()
    table[...] = index_table(corners, grid_slot, near, ix, iz, iy, ik)
    indices = pltpu.make_async_copy(table, tab, local.at[2])
    indices.start()

    inputs[3].wait()
    for s in range(SLOTS):
        for x, out, out_in in ((F - 1, planes_a, planes_a_in), (0, planes_b, planes_b_in)):
            rows = [fine[c, s, x : x + 1, h * 128 : h * 128 + 128] for c in range(3) for h in range(2)]
            tile = jnp.concatenate(rows, axis=0)
            out[s] = tile
            out_in[0, s] = tile
    pl.semaphore_wait(barrier, len(greeted))
    planes_copies = (
        gather(planes_a, planes_a_in, plane_peers, 0),
        gather(planes_b, planes_b_in, line_peers, 1),
    )

    indices.wait()
    for copy in loads + inputs[4:]:
        copy.wait()
    flat = brick.reshape(2 * 3 * 32 * PITCH, 128)
    lane = lax.broadcasted_iota(jnp.int32, (1, 128), 1)
    sub = lax.broadcasted_iota(jnp.int32, (8, 128), 0)

    def cut(dy, core, rows, out):
        mid, left, right = (Window(tab, flat, dy, core, dx) for dx in (0, -1, 1))
        body = jnp.zeros((32, 128), jnp.float32)
        low = jnp.zeros((1, 128), jnp.float32)
        high = jnp.zeros((1, 128), jnp.float32)
        for c, yy, base in rows:
            body += mid.row(c, yy, base)
            low += right.row(c, yy, base, 31)
            high += left.row(c, yy, base, 0)
        out[0:32, :] = body
        out[32:40, :] = jnp.where(sub == 0, low, jnp.where(sub == 1, high, 0.0))

    first = []
    for n, to in y_peers:
        dy, core = beside_of[n]
        cut(dy, core, [(c, 9 if dy < 0 else 0, c * 10) for c in range(3)], beside.at[n])
        first.append(send(beside.at[n], near_y.at[n], y_send.at[n], y_recv.at[n], to))
    for core, out in ((1, other), (0, own)):
        for c in range(3):
            cut(0, core, [(c, yy, yy * 10) for yy in range(10)], out.at[c])
        if core:
            first.append(send(other, near_z, y_send.at[4], y_recv.at[4], partner))
    arrive(first)
    upper = near_y[0] + near_y[1]
    lower = near_y[2] + near_y[3]
    window = []
    for c in range(3):
        cells = own[c] + near_z[c]
        cells += jnp.where((lane >= 90) & (lane < 100), pltpu.roll(upper, 90 - 10 * c, 1), 0.0)
        cells += jnp.where(lane < 10, pltpu.roll(lower, (128 - 10 * c) % 128, 1), 0.0)
        window.append(cells)
        edge[c] = cells[32:40]
    x_copies = [send(edge, edges.at[n], x_send.at[n], x_recv.at[n], to) for n, to in x_peers]

    def tiles(row, offset, source):
        def take(n, out):
            for s in range(SLOTS):
                at = tab[row, offset + n * SLOTS + s]
                out[s] = source[at // SLOTS, at % SLOTS]

        return take

    def blocks(offset, source):
        def take(n, out):
            out[...] = source[tab[T_GHOST, offset + n * SLOTS]]

        return take

    arrive(planes_copies[0])
    planes_copies += (passed(tiles(T_PLANE, 0, planes_a_in), planes_a_to, planes_a_at, line_peers, 0),)
    arrive(planes_copies[1])
    planes_copies += (passed(tiles(T_PLANE, 32, planes_b_in), planes_b_to, planes_b_at, plane_peers, 1),)

    arrive(x_copies)
    total = jnp.zeros((40, 128), jnp.float32)
    ends = jnp.zeros((8, 128), jnp.float32)
    for c in range(3):
        from_low = jnp.where(chain > 0, edges[0, c], 0.0)
        from_high = jnp.where(chain < 31, edges[1, c], 0.0)
        tile = jnp.where(sub == 0, from_low, jnp.where(sub == 1, from_high, 0.0))
        body = window[c][0:32]
        total += dot_right(jnp.concatenate([body, tile], axis=0), side[c])
        low = 0.75 * tile[0:1] + 0.25 * body[0:1]
        high = 0.75 * tile[1:2] + 0.25 * body[31:32]
        ends += jnp.where(sub == 2 + 2 * c, low, jnp.where(sub == 3 + 2 * c, high, 0.0))
    last = jnp.concatenate([total[24:32], jnp.where(sub < 2, total[32:40], ends)], axis=0)
    ghost_a[...] = total[0:24]
    ghost_a_in[0] = total[0:24]
    ghost_b[...] = last
    ghost_b_in[0] = last
    copies_a = gather(ghost_a, ghost_a_in, plane_peers, 2)
    copies_b = gather(ghost_b, ghost_b_in, line_peers, 3)
    arrive(copies_a)
    ghost_copies = passed(blocks(0, ghost_a_in), ghost_a_to, ghost_a_at, line_peers, 2)
    arrive(copies_b)
    ghost_copies += passed(blocks(32, ghost_b_in), ghost_b_to, ghost_b_at, plane_peers, 3)
    arrive(planes_copies[2])
    arrive(planes_copies[3])
    arrive(ghost_copies)

    block = jnp.concatenate([ghost_a_at[tab[T_GHOST_AT, 0]], ghost_b_at[tab[T_GHOST_AT, 32]]], axis=0)
    pulled = dot_right(dot_left(along[...], block), spread[...])
    for q in range(SLOTS):
        pull[q] = pulled[q * F : q * F + F]
    faces = dot_right(block[32:40], face[...])

    lane = lax.broadcasted_iota(jnp.int32, (F, F * F), 1)
    row = lax.broadcasted_iota(jnp.int32, (F, F * F), 0)
    for s in range(SLOTS):
        rate = RATE * visc[s]
        ghosts = pull[tab[T_BOX, s]]
        active = tab[T_ACTIVE, s] > 0
        planes = (planes_a_at[tab[T_PLANE_AT, s], s], planes_b_at[tab[T_PLANE_AT, 32 + s], s])
        has_near = (tab[T_NEAR, s] > 0, tab[T_NEAR, 32 + s] > 0)
        for c in range(3):
            cells = fine[c, s]
            ends = [
                jnp.where(
                    has_near[d],
                    jnp.concatenate([planes[d][2 * c : 2 * c + 1], planes[d][2 * c + 1 : 2 * c + 2]], axis=1),
                    faces[2 + 2 * c + d : 3 + 2 * c + d],
                )
                for d in range(2)
            ]
            around = ghosts[:, c * F * F : (c + 1) * F * F] - 6.0 * cells
            around += jnp.where(row == 0, ends[0], pltpu.roll(cells, 1, 0))
            around += jnp.where(row == F - 1, ends[1], pltpu.roll(cells, F - 1, 0))
            around += jnp.where(lane < F, 0.0, pltpu.roll(cells, F, 1))
            around += jnp.where(lane >= F * F - F, 0.0, pltpu.roll(cells, F * F - F, 1))
            around += jnp.where(lane % F == 0, 0.0, pltpu.roll(cells, 1, 1))
            around += jnp.where(lane % F == F - 1, 0.0, pltpu.roll(cells, F * F - 1, 1))
            moved = cells + rate * around
            result[c, s] = jnp.where(active, moved, 0.0)
            adv[(c * SLOTS + s) * F : (c * SLOTS + s + 1) * F, :] = moved

    summed = dot_right(adv[...], pair_yz[...])
    mean = dot_left(pair_x[0], summed[:, 0:128]) + dot_left(pair_x[1], summed[:, 128:256])
    for s in range(SLOTS):
        for part, (out, out_in) in enumerate(((means_a, means_a_in), (means_b, means_b_in))):
            tile = mean[part * 32 + s * 8 : part * 32 + s * 8 + 6]
            out[s] = tile
            out_in[0, s] = tile
    facts = (tab[T_Y, 9], tab[T_Z, 9], tab[T_HERE, 0])
    facts = sum(jnp.where(lane[0:1] == n, v.astype(jnp.float32), 0.0) for n, v in enumerate(facts))
    result[2, SLOTS, 0:1, :] = facts
    copies_a = gather(means_a, means_a_in, plane_peers, 4)
    copies_b = gather(means_b, means_b_in, line_peers, 5)
    arrive(copies_a)
    means_copies = passed(tiles(T_MEAN, 0, means_a_in), means_a_to, means_a_at, line_peers, 4)
    arrive(copies_b)
    means_copies += passed(tiles(T_MEAN, 32, means_b_in), means_b_to, means_b_at, plane_peers, 5)
    arrive(means_copies)
    for q in range(SLOTS):
        spot = (SLOTS, slice(q // 2 * 8, q // 2 * 8 + 6), slice(q % 2 * 128, q % 2 * 128 + 128))
        result[0, *spot] = means_a_at[tab[T_MEAN_AT, q], q]
        result[1, *spot] = means_b_at[tab[T_MEAN_AT, 32 + q], q]
    for copy in started:
        copy.wait_send()


def place_kernel(result, coarse, fine_out, out, brick, in_sems, out_sems):
    reads = [pltpu.make_async_copy(coarse.at[c], brick.at[c], in_sems.at[c]) for c in range(3)]
    for copy in reads:
        copy.start()
    writes = [pltpu.make_async_copy(result.at[:, 0:SLOTS], fine_out, out_sems.at[3])]
    writes[0].start()
    lane = lax.broadcasted_iota(jnp.int32, (8, 128), 1)
    facts = result[2, SLOTS, 0:1, 0:128]
    y, z, here = (jnp.sum(jnp.where(lane[0:1] == n, facts, 0.0)).astype(jnp.int32) for n in range(3))
    shift = z & 127
    here = here > 0
    keep = (lane >= shift) & (lane < shift + 8) & here
    y = pl.multiple_of(y, 8)
    z = pl.multiple_of(z - shift, 128)
    for c in range(3):
        reads[c].wait()
        for q in range(SLOTS):
            for a in range(B):
                r = 2 * c + a // 2 % 2
                r += q // 2 * 8
                line = result[a // 4, SLOTS, r : r + 1, q % 2 * 128 : q % 2 * 128 + 128]
                line = jnp.broadcast_to(line, (8, 128))
                line = pltpu.roll(pltpu.roll(line, 72 - 64 * (a % 2), 1, stride=8, stride_axis=0), shift, 1)
                spot = (c, q * B + a, pl.ds(y, 8), pl.ds(z, 128))
                brick[spot] = jnp.where(keep, line, brick[spot])
        copy = pltpu.make_async_copy(brick.at[c], out.at[c], out_sems.at[c])
        copy.start()
        writes.append(copy)
    for copy in writes:
        copy.wait()


def spec(space):
    return pl.BlockSpec(memory_space=space)


def on_device(coarse, fine, visc, corners, grid_slot, neighbors):
    f32 = jnp.float32
    dma = pltpu.SemaphoreType.DMA
    weights = [jnp.asarray(v, jnp.bfloat16) for v in constants()]
    tiles, a, b = (SLOTS, 6, 128), (24, 128), (16, 128)
    sides = (tiles, tiles, a, b, tiles, tiles)
    gathered = [((PLANE, LINE)[n % 2],) + shape for n, shape in enumerate(sides)]
    onward = [((LINE, PLANE)[n % 2],) + shape for n, shape in enumerate(sides)]
    result = pl.pallas_call(
        exchange_kernel,
        out_shape=jax.ShapeDtypeStruct((3, SLOTS + 1, F, F * F), f32),
        in_specs=[spec(pltpu.HBM)] * (6 + len(weights)),
        out_specs=spec(VMEM),
        scratch_shapes=[
            VMEM((3, corners.shape[0]), jnp.int32),
            VMEM((1, corners.shape[0]), jnp.int32),
            VMEM((2, corners.shape[0]), jnp.int32),
            VMEM(fine.shape, f32),
            VMEM(visc.shape, f32),
        ]
        + [VMEM(w.shape, w.dtype) for w in weights]
        + [
            VMEM((T_ROWS, 128), jnp.int32),
            pltpu.SMEM((T_ROWS, 128), jnp.int32),
            VMEM((2, 3, 32, PITCH, 128), f32),
            VMEM((3, 40, 128), f32),
            VMEM((3, 40, 128), f32),
            VMEM((4, 40, 128), f32),
            VMEM((3, 40, 128), f32),
            VMEM((4, 40, 128), f32),
            VMEM((3, 8, 128), f32),
            VMEM((2, 3, 8, 128), f32),
            VMEM((SLOTS, F, 3 * F * F), f32),
            VMEM((3 * SLOTS * F, F * F), f32),
        ]
        + [VMEM(shape, f32) for shape in (*sides, *gathered, *onward, *onward)]
        + [dma((5 + len(weights),)), dma((3,)), dma((5,)), dma((5,)), dma((2,)), dma((2,))]
        + [dma((6, PLANE))] * 4,
        compiler_params=pltpu.CompilerParams(collective_id=1, has_side_effects=True),
        name="exchange",
    )(
        corners.T, grid_slot.reshape(1, -1), neighbors.T, coarse, fine, visc,
        *weights,
    )
    return pl.pallas_call(
        place_kernel,
        out_shape=(jax.ShapeDtypeStruct(fine.shape, f32), jax.ShapeDtypeStruct(coarse.shape, f32)),
        in_specs=[spec(VMEM), spec(pl.ANY)],
        out_specs=(spec(pl.ANY), spec(pl.ANY)),
        scratch_shapes=[VMEM(coarse.shape, f32), dma((3,)), dma((4,))],
        compiler_params=pltpu.CompilerParams(vmem_limit_bytes=16 << 20),
        name="place",
    )(result, coarse)


def solution(mesh):
    split = Mesh(
        mesh.devices.reshape(NXC, NZC, mesh.shape["gy"], mesh.shape["gz"]), ("gx_0", "gx_1", "gy", "gz")
    )
    in_specs = (
        P(None, GX, "gy", "gz"),
        P(None, GX_GY_GZ, None, None),
        P(GX_GY_GZ, None, None),
        P(),
        P(),
        P(),
    )
    out_specs = (P(None, GX_GY_GZ, None, None), P(None, GX, "gy", "gz"))
    return jax.shard_map(on_device, mesh=split, in_specs=in_specs, out_specs=out_specs, check_vma=False)
```

time: 71.4 us -> 47.8 us (0.67)
  the two profiles are of different devices: /device:TPU:16 before, /device:TPU:8 now
where the time goes in v2:
time: 47.8 us; the launch traced here: 47.5 us
  Pallas kernels  45.9 us (96%)
  local copies, waits for them, and re-layouts  0.94 us (2%)
  between operations  0.66 us (1%)
    pallas_call x1, Pallas kernels, on_device(): pl.pallas_call(exchange_kernel, out_shape=jax.ShapeDtypeStruct((3, SLOTS...  43.7 us
    pallas_call x1, Pallas kernels, on_device(): pl.pallas_call(place_kernel, out_shape=(jax.ShapeDtypeStruct(fine.shape,...  2.23 us

profile of v2, /device:TPU:8, one launch (start us, length us, event | category | flops | bytes accessed | tf_op | source)
XLA Modules:
  0.0 47.5 jit_solution(1442358255403017414)
XLA Ops:
  0.6 0.0 copy-start
  0.6 43.7 %exchange.1.result = f32[3,5,16,256]{3,2,1,0:T(8,128)} custom-call(s32[3,512]{1,0:T(4,128)} %bitcast.3, s32[1,512]{1,0:T(1,128)} %bitcast.5, s32[2,512]{1,0:T(2,128)} %bitcast.4, f32[3,32,32,256]{3,2,1,0:T(8,128)} %coarse.3, f32[3,4,16,256]{3,2,1,0:T(8,128)} %fine_in.1, f32[4,16,256]{2,1,0:T(8,128)} %visc_in.1, bf16[3,128,128]{2,1,0:T(8,128)(2,1)} %constant.12.clone.side_in, ...), custom_call_target="tpu_custom_call" | custom-call | tf_op jit(solution)/shard_map/exchange/pallas_call | solution.py:520
  44.3 0.0 copy-done
  44.3 0.0 copy-start.1
  44.3 0.9 %copy-done.1 = f32[3,5,16,256]{3,2,1,0:T(8,128)S(1)} copy-done((f32[3,5,16,256]{3,2,1,0:T(8,128)S(1)}, f32[3,5,16,256]{3,2,1,0:T(8,128)}, u32[]{:S(2)}) %copy-start.1) | copy-done | bytes 245784
  45.3 2.2 %place.1 = (f32[3,4,16,256]{3,2,1,0:T(8,128)}, f32[3,32,32,256]{3,2,1,0:T(8,128)}) custom-call(f32[3,5,16,256]{3,2,1,0:T(8,128)S(1)} %copy-done.1, f32[3,32,32,256]{3,2,1,0:T(8,128)S(1)} %copy-done), custom_call_target="tpu_custom_call" | custom-call | tf_op jit(solution)/shard_map/place/pallas_call | solution.py:556
Async XLA Ops:
  0.6 43.7 %copy-start = (f32[3,32,32,256]{3,2,1,0:T(8,128)S(1)}, f32[3,32,32,256]{3,2,1,0:T(8,128)}, u32[]{:S(2)}) copy-start(f32[3,32,32,256]{3,2,1,0:T(8,128)} %coarse.3) | copy-start | bytes 9437188
  44.3 0.9 %copy-start.1 = (f32[3,5,16,256]{3,2,1,0:T(8,128)S(1)}, f32[3,5,16,256]{3,2,1,0:T(8,128)}, u32[]{:S(2)}) copy-start(f32[3,5,16,256]{3,2,1,0:T(8,128)} %exchange.1.result) | copy-start | bytes 737284

commit v3 on v2

--- a/solution.py
+++ b/solution.py
@@ -28,9 +28,9 @@
 T_ACTIVE = 7
 T_BOX = 8
 T_HERE = 9
-T_Y = 10
-T_Z = 11
 T_ROWS = 16
+W_Y, W_Z = 0, 1
+W_ROWS = 8
 LINE, PLANE = NZC, NXC * NYC
 
 
@@ -94,18 +94,40 @@
     )
 
 
+def pick(mask, value):
+    return jnp.max(jnp.where(mask, value, -1), axis=1, keepdims=True)
+
+
+def brick_of(corners):
+    return ((corners[0:1] >> 5) * NYC + (corners[1:2] >> 5)) * 2 + (corners[2:3] >> 8)
+
+
+def as_rows(columns, rows):
+    lane = lax.broadcasted_iota(jnp.int32, (1, 128), 1)
+    table = jnp.zeros((128, 128), jnp.int32)
+    for j, column in enumerate(columns):
+        column = jnp.concatenate([column, jnp.zeros((128 - column.shape[0], 1), jnp.int32)], axis=0)
+        table = jnp.where(lane == j, column, table)
+    return table.T[0:rows]
+
+
+def window_table(corners, ix, iz, iy, ik):
+    place = (corners[1:2] & 31) * 256 + (corners[2:3] & 255)
+    n = lax.broadcasted_iota(jnp.int32, (24, 1), 0)
+    x = (ix * NZC + iz + (n & 3) - 1) & 31
+    y = (iy + (n >> 3) - 1) & 3
+    k = (ik + (n >> 2)) & 1
+    found = jnp.maximum(pick((x * NYC + y) * 2 + k == brick_of(corners), place), 0)
+    return as_rows([(found >> 8) + (y - iy) * 32, (found & 255) + (k - ik) * 256], W_ROWS)
+
+
 def index_table(corners, grid_slot, near, ix, iz, iy, ik):
     i32 = jnp.int32
     gs = grid_slot[...]
-    cx, cy, cz = corners[0:1], corners[1:2], corners[2:3]
-    brick = ((cx >> 5) * NYC + (cy >> 5)) * 2 + (cz >> 8)
-    box = (cx >> 3) & 3
-    place = (cy & 31) * 256 + (cz & 255)
+    brick = brick_of(corners)
+    box = (corners[0:1] >> 3) & 3
     total = gs.shape[1]
     grids = lax.broadcasted_iota(i32, (1, total), 1)
-
-    def pick(mask, value):
-        return jnp.max(jnp.where(mask, value, -1), axis=1, keepdims=True)
 
     def lies(n):
         return n >> 6, (n >> 3) & 7, (n >> 1) & 3
@@ -161,26 +183,13 @@
         lambda o: ((((ix + (o >> 2)) & 3) * NZC + iz) * NYC + ((iy + o) & 3)) * 2 + ik,
         1, line_gather, plane_at,
     )
-    n = lax.broadcasted_iota(i32, (24, 1), 0)
-    x = (ix * NZC + iz + (n & 3) - 1) & 31
-    y = (iy + (n >> 3) - 1) & 3
-    k = (ik + (n >> 2)) & 1
-    found = jnp.maximum(pick((x * NYC + y) * 2 + k == brick, place), 0)
-    lane = lax.broadcasted_iota(i32, (1, 128), 1)
-    rest = jnp.zeros((128 - 24, 1), i32)
-    columns = [jnp.concatenate([a, b, jnp.zeros((32, 1), i32)], axis=0) for a, b in zip(along, across)]
-    columns.append(jnp.concatenate([(found >> 8) + (y - iy) * 32, rest], axis=0))
-    columns.append(jnp.concatenate([(found & 255) + (k - ik) * 256, rest], axis=0))
-    table = jnp.zeros((128, 128), i32)
-    for j, column in enumerate(columns):
-        table = jnp.where(lane == j, column, table)
-    return table.T[0:T_ROWS]
+    return as_rows([jnp.concatenate([a, b], axis=0) for a, b in zip(along, across)], T_ROWS)
 
 
 class Window:
     def __init__(self, tab, flat, dy, core, dx):
         at = (dy + 1) * 8 + core * 4 + dx + 1
-        self.flat, self.y, self.z = flat, tab[T_Y, at], tab[T_Z, at]
+        self.flat, self.y, self.z = flat, tab[W_Y, at], tab[W_Z, at]
         z = self.z & 255
         self.half, shift = z >> 7, z & 127
         self.first = (shift - 1) & 127
@@ -226,7 +235,7 @@
     pair_yz_in, pair_x_in,
     result,
     corners, grid_slot, near, fine, visc, side, along, spread, face, pair_yz, pair_x,
-    table, tab, brick, own, other, beside, near_z, near_y, edge, edges, pull, adv,
+    table, tab, places, spots, brick, own, other, beside, near_z, near_y, edge, edges, pull, adv,
     planes_a, planes_b, ghost_a, ghost_b, means_a, means_b,
     planes_a_in, planes_b_in, ghost_a_in, ghost_b_in, means_a_in, means_b_in,
     planes_a_to, planes_b_to, ghost_a_to, ghost_b_to, means_a_to, means_b_to,
@@ -250,13 +259,19 @@
         (n, device(ix, (iz + n) % NZC, iy, ik)) for n in sorted(range(1, LINE), key=lambda n: -far(n, NZC))
     ]
     chain = ix * NZC + iz
-    up, down = (chain + 1) % 32, (chain + 31) % 32
-    x_peers = [(0, device(up // NZC, up % NZC, iy, ik)), (1, device(down // NZC, down % NZC, iy, ik))]
     beside_of = ((-1, 0), (-1, 1), (1, 0), (1, 1))
     y_peers = [
         (n, device(ix, iz, (iy + dy) % NYC, (ik + dk) % 2)) for n, (dy, dk) in enumerate(beside_of)
     ]
     partner = device(ix, iz, iy, 1 - ik)
+    around_of = [(dy, core) for dy in (-1, 1, 0) for core in (0, 1)]
+    edge_peers = []
+    for side_x, step in enumerate((1, 31)):
+        x = (chain + step) % 32
+        for n, (dy, core) in enumerate(around_of):
+            edge_peers.append(
+                (side_x * 6 + n, device(x // NZC, x % NZC, (iy + dy) % NYC, (ik + core) % 2))
+            )
     started = []
 
     def send(src, dst, send_sem, recv_sem, to):
@@ -303,15 +318,14 @@
     for copy in inputs[:4] + loads + inputs[4:]:
         copy.start()
     barrier = pltpu.get_barrier_semaphore()
-    greeted = plane_peers + line_peers + x_peers + [y_peers[1], y_peers[3], (0, partner)]
+    greeted = plane_peers + line_peers + edge_peers + [y_peers[1], y_peers[3], (0, partner)]
     for _, to in greeted:
         pl.semaphore_signal(barrier, inc=1, device_id=to, device_id_type=MESH)
 
-    for copy in inputs[:3]:
-        copy.wait()
-    table[...] = index_table(corners, grid_slot, near, ix, iz, iy, ik)
-    indices = pltpu.make_async_copy(table, tab, local.at[2])
-    indices.start()
+    inputs[0].wait()
+    places[...] = window_table(corners, ix, iz, iy, ik)
+    indices = [pltpu.make_async_copy(places, spots, local.at[2]), pltpu.make_async_copy(table, tab, local.at[3])]
+    indices[0].start()
 
     inputs[3].wait()
     for s in range(SLOTS):
@@ -326,7 +340,7 @@
         gather(planes_b, planes_b_in, line_peers, 1),
     )
 
-    indices.wait()
+    indices[0].wait()
     for copy in loads + inputs[4:]:
         copy.wait()
     flat = brick.reshape(2 * 3 * 32 * PITCH, 128)
@@ -334,69 +348,53 @@
     sub = lax.broadcasted_iota(jnp.int32, (8, 128), 0)
 
     def cut(dy, core, rows, out):
-        mid, left, right = (Window(tab, flat, dy, core, dx) for dx in (0, -1, 1))
-        body = jnp.zeros((32, 128), jnp.float32)
-        low = jnp.zeros((1, 128), jnp.float32)
-        high = jnp.zeros((1, 128), jnp.float32)
-        for c, yy, base in rows:
-            body += mid.row(c, yy, base)
-            low += right.row(c, yy, base, 31)
-            high += left.row(c, yy, base, 0)
-        out[0:32, :] = body
-        out[32:40, :] = jnp.where(sub == 0, low, jnp.where(sub == 1, high, 0.0))
+        mid = Window(spots, flat, dy, core, 0)
+        out[...] = sum(mid.row(c, yy, base) for c, yy, base in rows)
+
+    def cut_edges(n, dy, core):
+        for side_x, x in enumerate((31, 0)):
+            window = Window(spots, flat, dy, core, 1 - 2 * side_x)
+            tile = jnp.zeros((8, 128), jnp.float32)
+            for c in range(3):
+                lines = [(9,), (0,), range(10)][(-1, 1, 0).index(dy)]
+                line = sum(window.row(c, yy, yy * 10, x) for yy in lines)
+                tile = jnp.where(sub == c, line, tile)
+            edge[side_x * 6 + n] = tile
 
     first = []
     for n, to in y_peers:
         dy, core = beside_of[n]
         cut(dy, core, [(c, 9 if dy < 0 else 0, c * 10) for c in range(3)], beside.at[n])
         first.append(send(beside.at[n], near_y.at[n], y_send.at[n], y_recv.at[n], to))
+    for n, (dy, core) in enumerate(around_of):
+        cut_edges(n, dy, core)
+        for at in (n, 6 + n):
+            first.append(send(edge.at[at], edges.at[at], x_send.at[at], x_recv.at[at], edge_peers[at][1]))
     for core, out in ((1, other), (0, own)):
         for c in range(3):
             cut(0, core, [(c, yy, yy * 10) for yy in range(10)], out.at[c])
         if core:
             first.append(send(other, near_z, y_send.at[4], y_recv.at[4], partner))
+    for copy in inputs[1:3]:
+        copy.wait()
+    table[...] = index_table(corners, grid_slot, near, ix, iz, iy, ik)
+    indices[1].start()
     arrive(first)
     upper = near_y[0] + near_y[1]
     lower = near_y[2] + near_y[3]
-    window = []
-    for c in range(3):
-        cells = own[c] + near_z[c]
-        cells += jnp.where((lane >= 90) & (lane < 100), pltpu.roll(upper, 90 - 10 * c, 1), 0.0)
-        cells += jnp.where(lane < 10, pltpu.roll(lower, (128 - 10 * c) % 128, 1), 0.0)
-        window.append(cells)
-        edge[c] = cells[32:40]
-    x_copies = [send(edge, edges.at[n], x_send.at[n], x_recv.at[n], to) for n, to in x_peers]
-
-    def tiles(row, offset, source):
-        def take(n, out):
-            for s in range(SLOTS):
-                at = tab[row, offset + n * SLOTS + s]
-                out[s] = source[at // SLOTS, at % SLOTS]
-
-        return take
-
-    def blocks(offset, source):
-        def take(n, out):
-            out[...] = source[tab[T_GHOST, offset + n * SLOTS]]
-
-        return take
-
-    arrive(planes_copies[0])
-    planes_copies += (passed(tiles(T_PLANE, 0, planes_a_in), planes_a_to, planes_a_at, line_peers, 0),)
-    arrive(planes_copies[1])
-    planes_copies += (passed(tiles(T_PLANE, 32, planes_b_in), planes_b_to, planes_b_at, plane_peers, 1),)
-
-    arrive(x_copies)
+    from_low = jnp.where(chain > 0, sum(edges[n] for n in range(6)), 0.0)
+    from_high = jnp.where(chain < 31, sum(edges[n] for n in range(6, 12)), 0.0)
     total = jnp.zeros((40, 128), jnp.float32)
     ends = jnp.zeros((8, 128), jnp.float32)
     for c in range(3):
-        from_low = jnp.where(chain > 0, edges[0, c], 0.0)
-        from_high = jnp.where(chain < 31, edges[1, c], 0.0)
-        tile = jnp.where(sub == 0, from_low, jnp.where(sub == 1, from_high, 0.0))
-        body = window[c][0:32]
+        body = own[c] + near_z[c]
+        body += jnp.where((lane >= 90) & (lane < 100), pltpu.roll(upper, 90 - 10 * c, 1), 0.0)
+        body += jnp.where(lane < 10, pltpu.roll(lower, (128 - 10 * c) % 128, 1), 0.0)
+        low, high = from_low[c : c + 1], from_high[c : c + 1]
+        tile = jnp.where(sub == 0, low, jnp.where(sub == 1, high, 0.0))
         total += dot_right(jnp.concatenate([body, tile], axis=0), side[c])
-        low = 0.75 * tile[0:1] + 0.25 * body[0:1]
-        high = 0.75 * tile[1:2] + 0.25 * body[31:32]
+        low = 0.75 * low + 0.25 * body[0:1]
+        high = 0.75 * high + 0.25 * body[31:32]
         ends += jnp.where(sub == 2 + 2 * c, low, jnp.where(sub == 3 + 2 * c, high, 0.0))
     last = jnp.concatenate([total[24:32], jnp.where(sub < 2, total[32:40], ends)], axis=0)
     ghost_a[...] = total[0:24]
@@ -405,6 +403,27 @@
     ghost_b_in[0] = last
     copies_a = gather(ghost_a, ghost_a_in, plane_peers, 2)
     copies_b = gather(ghost_b, ghost_b_in, line_peers, 3)
+    indices[1].wait()
+
+    def tiles(row, offset, source):
+        def take(n, out):
+            for s in range(SLOTS):
+                at = tab[row, offset + n * SLOTS + s]
+                out[s] = source[at // SLOTS, at % SLOTS]
+
+        return take
+
+    def blocks(offset, source):
+        def take(n, out):
+            out[...] = source[tab[T_GHOST, offset + n * SLOTS]]
+
+        return take
+
+    arrive(planes_copies[0])
+    planes_copies += (passed(tiles(T_PLANE, 0, planes_a_in), planes_a_to, planes_a_at, line_peers, 0),)
+    arrive(planes_copies[1])
+    planes_copies += (passed(tiles(T_PLANE, 32, planes_b_in), planes_b_to, planes_b_at, plane_peers, 1),)
+
     arrive(copies_a)
     ghost_copies = passed(blocks(0, ghost_a_in), ghost_a_to, ghost_a_at, line_peers, 2)
     arrive(copies_b)
@@ -455,7 +474,7 @@
             tile = mean[part * 32 + s * 8 : part * 32 + s * 8 + 6]
             out[s] = tile
             out_in[0, s] = tile
-    facts = (tab[T_Y, 9], tab[T_Z, 9], tab[T_HERE, 0])
+    facts = (spots[W_Y, 9], spots[W_Z, 9], tab[T_HERE, 0])
     facts = sum(jnp.where(lane[0:1] == n, v.astype(jnp.float32), 0.0) for n, v in enumerate(facts))
     result[2, SLOTS, 0:1, :] = facts
     copies_a = gather(means_a, means_a_in, plane_peers, 4)
@@ -533,19 +552,21 @@
         + [
             VMEM((T_ROWS, 128), jnp.int32),
             pltpu.SMEM((T_ROWS, 128), jnp.int32),
+            VMEM((W_ROWS, 128), jnp.int32),
+            pltpu.SMEM((W_ROWS, 128), jnp.int32),
             VMEM((2, 3, 32, PITCH, 128), f32),
-            VMEM((3, 40, 128), f32),
-            VMEM((3, 40, 128), f32),
-            VMEM((4, 40, 128), f32),
-            VMEM((3, 40, 128), f32),
-            VMEM((4, 40, 128), f32),
-            VMEM((3, 8, 128), f32),
-            VMEM((2, 3, 8, 128), f32),
+            VMEM((3, 32, 128), f32),
+            VMEM((3, 32, 128), f32),
+            VMEM((4, 32, 128), f32),
+            VMEM((3, 32, 128), f32),
+            VMEM((4, 32, 128), f32),
+            VMEM((12, 8, 128), f32),
+            VMEM((12, 8, 128), f32),
             VMEM((SLOTS, F, 3 * F * F), f32),
             VMEM((3 * SLOTS * F, F * F), f32),
         ]
         + [VMEM(shape, f32) for shape in (*sides, *gathered, *onward, *onward)]
-        + [dma((5 + len(weights),)), dma((3,)), dma((5,)), dma((5,)), dma((2,)), dma((2,))]
+        + [dma((5 + len(weights),)), dma((4,)), dma((5,)), dma((5,)), dma((12,)), dma((12,))]
         + [dma((6, PLANE))] * 4,
         compiler_params=pltpu.CompilerParams(collective_id=1, has_side_effects=True),
         name="exchange",

time: 47.8 us -> 46.1 us (0.964)
  Pallas kernels: 45.9 us -> 44.2 us
    pallas_call x1, Pallas kernels: 43.7 us -> 42 us  [on_device(): pl.pallas_call(exchange_kernel, out_shape=jax.ShapeDtypeStruct((3, SLOTS...]
where the time goes in v3:
time: 46.1 us; the launch traced here: 45.8 us
  Pallas kernels  44.2 us (96%)
  local copies, waits for them, and re-layouts  0.94 us (2%)
  between operations  0.66 us (1%)
    pallas_call x1, Pallas kernels, on_device(): pl.pallas_call(exchange_kernel, out_shape=jax.ShapeDtypeStruct((3, SLOTS...  42 us
    pallas_call x1, Pallas kernels, on_device(): pl.pallas_call(place_kernel, out_shape=(jax.ShapeDtypeStruct(fine.shape,...  2.23 us
    unnamed x4, local copies, waits for them, and re-layouts  0.94 us

profile of v3, /device:TPU:8, one launch (start us, length us, event | category | flops | bytes accessed | tf_op | source)
XLA Modules:
  0.0 45.8 jit_solution(9610092898220692269)
XLA Ops:
  0.6 0.0 copy-start
  0.6 42.0 %exchange.1.result = f32[3,5,16,256]{3,2,1,0:T(8,128)} custom-call(s32[3,512]{1,0:T(4,128)} %bitcast.3, s32[1,512]{1,0:T(1,128)} %bitcast.5, s32[2,512]{1,0:T(2,128)} %bitcast.4, f32[3,32,32,256]{3,2,1,0:T(8,128)} %coarse.3, f32[3,4,16,256]{3,2,1,0:T(8,128)} %fine_in.1, f32[4,16,256]{2,1,0:T(8,128)} %visc_in.1, bf16[3,128,128]{2,1,0:T(8,128)(2,1)} %constant.12.clone.side_in, ...), custom_call_target="tpu_custom_call" | custom-call | tf_op jit(solution)/shard_map/exchange/pallas_call | solution.py:539
  42.6 0.0 copy-done
  42.6 0.0 copy-start.1
  42.6 0.9 %copy-done.1 = f32[3,5,16,256]{3,2,1,0:T(8,128)S(1)} copy-done((f32[3,5,16,256]{3,2,1,0:T(8,128)S(1)}, f32[3,5,16,256]{3,2,1,0:T(8,128)}, u32[]{:S(2)}) %copy-start.1) | copy-done | bytes 245784
  43.6 2.2 %place.1 = (f32[3,4,16,256]{3,2,1,0:T(8,128)}, f32[3,32,32,256]{3,2,1,0:T(8,128)}) custom-call(f32[3,5,16,256]{3,2,1,0:T(8,128)S(1)} %copy-done.1, f32[3,32,32,256]{3,2,1,0:T(8,128)S(1)} %copy-done), custom_call_target="tpu_custom_call" | custom-call | tf_op jit(solution)/shard_map/place/pallas_call | solution.py:577
Async XLA Ops:
  0.6 42.0 %copy-start = (f32[3,32,32,256]{3,2,1,0:T(8,128)S(1)}, f32[3,32,32,256]{3,2,1,0:T(8,128)}, u32[]{:S(2)}) copy-start(f32[3,32,32,256]{3,2,1,0:T(8,128)} %coarse.3) | copy-start | bytes 9437188
  42.6 0.9 %copy-start.1 = (f32[3,5,16,256]{3,2,1,0:T(8,128)S(1)}, f32[3,5,16,256]{3,2,1,0:T(8,128)}, u32[]{:S(2)}) copy-start(f32[3,5,16,256]{3,2,1,0:T(8,128)} %exchange.1.result) | copy-start | bytes 737284

commit v4 on v3

--- a/solution.py
+++ b/solution.py
@@ -252,25 +252,25 @@
         return min(n, count - n)
 
     plane_peers = [
-        (n, device((ix + n // NYC) % NXC, iz, (iy + n % NYC) % NYC, ik))
+        (n, device(lax.rem(ix + n // NYC, NXC), iz, lax.rem(iy + n % NYC, NYC), ik))
         for n in sorted(range(1, PLANE), key=lambda n: -far(n // NYC, NXC) - far(n % NYC, NYC))
     ]
     line_peers = [
-        (n, device(ix, (iz + n) % NZC, iy, ik)) for n in sorted(range(1, LINE), key=lambda n: -far(n, NZC))
+        (n, device(ix, lax.rem(iz + n, NZC), iy, ik)) for n in sorted(range(1, LINE), key=lambda n: -far(n, NZC))
     ]
     chain = ix * NZC + iz
     beside_of = ((-1, 0), (-1, 1), (1, 0), (1, 1))
     y_peers = [
-        (n, device(ix, iz, (iy + dy) % NYC, (ik + dk) % 2)) for n, (dy, dk) in enumerate(beside_of)
+        (n, device(ix, iz, lax.rem(iy + NYC + dy, NYC), lax.rem(ik + dk, 2))) for n, (dy, dk) in enumerate(beside_of)
     ]
     partner = device(ix, iz, iy, 1 - ik)
     around_of = [(dy, core) for dy in (-1, 1, 0) for core in (0, 1)]
     edge_peers = []
     for side_x, step in enumerate((1, 31)):
-        x = (chain + step) % 32
+        x = lax.rem(chain + step, 32)
         for n, (dy, core) in enumerate(around_of):
             edge_peers.append(
-                (side_x * 6 + n, device(x // NZC, x % NZC, (iy + dy) % NYC, (ik + core) % 2))
+                (side_x * 6 + n, device(lax.div(x, NZC), lax.rem(x, NZC), lax.rem(iy + NYC + dy, NYC), lax.rem(ik + core, 2)))
             )
     started = []
 
@@ -409,7 +409,7 @@
         def take(n, out):
             for s in range(SLOTS):
                 at = tab[row, offset + n * SLOTS + s]
-                out[s] = source[at // SLOTS, at % SLOTS]
+                out[s] = source[at >> 2, at & 3]
 
         return take
 
@@ -492,35 +492,39 @@
         copy.wait_send()
 
 
-def place_kernel(result, coarse, fine_out, out, brick, in_sems, out_sems):
-    reads = [pltpu.make_async_copy(coarse.at[c], brick.at[c], in_sems.at[c]) for c in range(3)]
-    for copy in reads:
-        copy.start()
-    writes = [pltpu.make_async_copy(result.at[:, 0:SLOTS], fine_out, out_sems.at[3])]
-    writes[0].start()
+def place_kernel(result, coarse, fine_out, out, column, sems):
+    fine_write = pltpu.make_async_copy(result.at[:, 0:SLOTS], fine_out, sems.at[8])
+    fine_write.start()
     lane = lax.broadcasted_iota(jnp.int32, (8, 128), 1)
     facts = result[2, SLOTS, 0:1, 0:128]
     y, z, here = (jnp.sum(jnp.where(lane[0:1] == n, facts, 0.0)).astype(jnp.int32) for n in range(3))
     shift = z & 127
-    here = here > 0
-    keep = (lane >= shift) & (lane < shift + 8) & here
+    keep = (lane >= shift) & (lane < shift + 8) & (here > 0)
+    mine = (y >> 3) * 2 + (z >> 7)
+    rest = []
+    for n in range(8):
+        part = (slice(None), slice(None), pl.ds(n // 2 * 8, 8), pl.ds(n % 2 * 128, 128))
+        rest.append(pltpu.make_async_copy(coarse.at[part], out.at[part], sems.at[n]))
+    for n in range(8):
+        pl.when(mine != n)(rest[n].start)
     y = pl.multiple_of(y, 8)
     z = pl.multiple_of(z - shift, 128)
+    writes = []
     for c in range(3):
-        reads[c].wait()
         for q in range(SLOTS):
             for a in range(B):
-                r = 2 * c + a // 2 % 2
-                r += q // 2 * 8
+                r = 2 * c + a // 2 % 2 + q // 2 * 8
                 line = result[a // 4, SLOTS, r : r + 1, q % 2 * 128 : q % 2 * 128 + 128]
                 line = jnp.broadcast_to(line, (8, 128))
                 line = pltpu.roll(pltpu.roll(line, 72 - 64 * (a % 2), 1, stride=8, stride_axis=0), shift, 1)
-                spot = (c, q * B + a, pl.ds(y, 8), pl.ds(z, 128))
-                brick[spot] = jnp.where(keep, line, brick[spot])
-        copy = pltpu.make_async_copy(brick.at[c], out.at[c], out_sems.at[c])
-        copy.start()
-        writes.append(copy)
-    for copy in writes:
+                old = coarse[c, q * B + a, pl.ds(y, 8), pl.ds(z, 128)]
+                column[c, q * B + a] = jnp.where(keep, line, old)
+        spot = out.at[c, :, pl.ds(y, 8), pl.ds(z, 128)]
+        writes.append(pltpu.make_async_copy(column.at[c], spot, sems.at[9 + c]))
+        writes[-1].start()
+    for n in range(8):
+        pl.when(mine != n)(rest[n].wait)
+    for copy in writes + [fine_write]:
         copy.wait()
 
 
@@ -577,9 +581,9 @@
     return pl.pallas_call(
         place_kernel,
         out_shape=(jax.ShapeDtypeStruct(fine.shape, f32), jax.ShapeDtypeStruct(coarse.shape, f32)),
-        in_specs=[spec(VMEM), spec(pl.ANY)],
+        in_specs=[spec(VMEM), spec(VMEM)],
         out_specs=(spec(pl.ANY), spec(pl.ANY)),
-        scratch_shapes=[VMEM(coarse.shape, f32), dma((3,)), dma((4,))],
+        scratch_shapes=[VMEM((3, 32, 8, 128), f32), dma((12,))],
         compiler_params=pltpu.CompilerParams(vmem_limit_bytes=16 << 20),
         name="place",
     )(result, coarse)

time: 46.1 us -> 45.5 us (0.987)
  Pallas kernels: 44.2 us -> 43.6 us
where the time goes in v4:
time: 45.5 us; the launch traced here: 45.2 us
  Pallas kernels  43.6 us (96%)
  local copies, waits for them, and re-layouts  0.94 us (2%)
  between operations  0.66 us (1%)
    pallas_call x1, Pallas kernels, on_device(): pl.pallas_call(exchange_kernel, out_shape=jax.ShapeDtypeStruct((3, SLOTS...  41.8 us
    pallas_call x1, Pallas kernels, on_device(): pl.pallas_call(place_kernel, out_shape=(jax.ShapeDtypeStruct(fine.shape,...  1.88 us
    unnamed x4, local copies, waits for them, and re-layouts  0.94 us

profile of v4, /device:TPU:8, one launch (start us, length us, event | category | flops | bytes accessed | tf_op | source)
XLA Modules:
  0.0 45.2 jit_solution(4677157856179833781)
XLA Ops:
  0.6 0.0 copy-start
  0.6 41.8 %exchange.1.result = f32[3,5,16,256]{3,2,1,0:T(8,128)} custom-call(s32[3,512]{1,0:T(4,128)} %bitcast.3, s32[1,512]{1,0:T(1,128)} %bitcast.5, s32[2,512]{1,0:T(2,128)} %bitcast.4, f32[3,32,32,256]{3,2,1,0:T(8,128)} %coarse.3, f32[3,4,16,256]{3,2,1,0:T(8,128)} %fine_in.1, f32[4,16,256]{2,1,0:T(8,128)} %visc_in.1, bf16[3,128,128]{2,1,0:T(8,128)(2,1)} %constant.12.clone.side_in, ...), custom_call_target="tpu_custom_call" | custom-call | tf_op jit(solution)/shard_map/exchange/pallas_call | solution.py:543
  42.4 0.0 copy-done
  42.4 0.0 copy-start.1
  42.4 0.9 %copy-done.1 = f32[3,5,16,256]{3,2,1,0:T(8,128)S(1)} copy-done((f32[3,5,16,256]{3,2,1,0:T(8,128)S(1)}, f32[3,5,16,256]{3,2,1,0:T(8,128)}, u32[]{:S(2)}) %copy-start.1) | copy-done | bytes 245784
  43.4 1.9 %place.1 = (f32[3,4,16,256]{3,2,1,0:T(8,128)}, f32[3,32,32,256]{3,2,1,0:T(8,128)}) custom-call(f32[3,5,16,256]{3,2,1,0:T(8,128)S(1)} %copy-done.1, f32[3,32,32,256]{3,2,1,0:T(8,128)S(1)} %copy-done), custom_call_target="tpu_custom_call" | custom-call | tf_op jit(solution)/shard_map/place/pallas_call | solution.py:581
Async XLA Ops:
  0.6 41.8 %copy-start = (f32[3,32,32,256]{3,2,1,0:T(8,128)S(1)}, f32[3,32,32,256]{3,2,1,0:T(8,128)}, u32[]{:S(2)}) copy-start(f32[3,32,32,256]{3,2,1,0:T(8,128)} %coarse.3) | copy-start | bytes 9437188
  42.4 0.9 %copy-start.1 = (f32[3,5,16,256]{3,2,1,0:T(8,128)S(1)}, f32[3,5,16,256]{3,2,1,0:T(8,128)}, u32[]{:S(2)}) copy-start(f32[3,5,16,256]{3,2,1,0:T(8,128)} %exchange.1.result) | copy-start | bytes 737284

commit v5 on v4

--- a/solution.py
+++ b/solution.py
@@ -335,10 +335,6 @@
             out[s] = tile
             out_in[0, s] = tile
     pl.semaphore_wait(barrier, len(greeted))
-    planes_copies = (
-        gather(planes_a, planes_a_in, plane_peers, 0),
-        gather(planes_b, planes_b_in, line_peers, 1),
-    )
 
     indices[0].wait()
     for copy in loads + inputs[4:]:
@@ -375,6 +371,10 @@
             cut(0, core, [(c, yy, yy * 10) for yy in range(10)], out.at[c])
         if core:
             first.append(send(other, near_z, y_send.at[4], y_recv.at[4], partner))
+    planes_copies = (
+        gather(planes_a, planes_a_in, plane_peers, 0),
+        gather(planes_b, planes_b_in, line_peers, 1),
+    )
     for copy in inputs[1:3]:
         copy.wait()
     table[...] = index_table(corners, grid_slot, near, ix, iz, iy, ik)

time: 45.5 us -> 45.2 us (level)
    pallas_call x1, Pallas kernels: 41.8 us -> 41.3 us  [on_device(): pl.pallas_call(exchange_kernel, out_shape=jax.ShapeDtypeStruct((3, SLOTS...]
where the time goes in v5:
time: 45.2 us; the launch traced here: 44.8 us
  Pallas kernels  43.2 us (96%)
  local copies, waits for them, and re-layouts  0.94 us (2%)
  between operations  0.66 us (1%)
    pallas_call x1, Pallas kernels, on_device(): pl.pallas_call(exchange_kernel, out_shape=jax.ShapeDtypeStruct((3, SLOTS...  41.3 us
    pallas_call x1, Pallas kernels, on_device(): pl.pallas_call(place_kernel, out_shape=(jax.ShapeDtypeStruct(fine.shape,...  1.88 us
    unnamed x4, local copies, waits for them, and re-layouts  0.94 us

profile of v5, /device:TPU:8, one launch (start us, length us, event | category | flops | bytes accessed | tf_op | source)
XLA Modules:
  0.0 44.8 jit_solution(6481585488247993107)
XLA Ops:
  0.6 0.0 copy-start
  0.6 41.3 %exchange.1.result = f32[3,5,16,256]{3,2,1,0:T(8,128)} custom-call(s32[3,512]{1,0:T(4,128)} %bitcast.3, s32[1,512]{1,0:T(1,128)} %bitcast.5, s32[2,512]{1,0:T(2,128)} %bitcast.4, f32[3,32,32,256]{3,2,1,0:T(8,128)} %coarse.3, f32[3,4,16,256]{3,2,1,0:T(8,128)} %fine_in.1, f32[4,16,256]{2,1,0:T(8,128)} %visc_in.1, bf16[3,128,128]{2,1,0:T(8,128)(2,1)} %constant.12.clone.side_in, ...), custom_call_target="tpu_custom_call" | custom-call | tf_op jit(solution)/shard_map/exchange/pallas_call | solution.py:543
  41.9 0.0 copy-done
  41.9 0.0 copy-start.1
  41.9 0.9 %copy-done.1 = f32[3,5,16,256]{3,2,1,0:T(8,128)S(1)} copy-done((f32[3,5,16,256]{3,2,1,0:T(8,128)S(1)}, f32[3,5,16,256]{3,2,1,0:T(8,128)}, u32[]{:S(2)}) %copy-start.1) | copy-done | bytes 245784
  42.9 1.9 %place.1 = (f32[3,4,16,256]{3,2,1,0:T(8,128)}, f32[3,32,32,256]{3,2,1,0:T(8,128)}) custom-call(f32[3,5,16,256]{3,2,1,0:T(8,128)S(1)} %copy-done.1, f32[3,32,32,256]{3,2,1,0:T(8,128)S(1)} %copy-done), custom_call_target="tpu_custom_call" | custom-call | tf_op jit(solution)/shard_map/place/pallas_call | solution.py:581
Async XLA Ops:
  0.6 41.3 %copy-start = (f32[3,32,32,256]{3,2,1,0:T(8,128)S(1)}, f32[3,32,32,256]{3,2,1,0:T(8,128)}, u32[]{:S(2)}) copy-start(f32[3,32,32,256]{3,2,1,0:T(8,128)} %coarse.3) | copy-start | bytes 9437188
  41.9 0.9 %copy-start.1 = (f32[3,5,16,256]{3,2,1,0:T(8,128)S(1)}, f32[3,5,16,256]{3,2,1,0:T(8,128)}, u32[]{:S(2)}) copy-start(f32[3,5,16,256]{3,2,1,0:T(8,128)} %exchange.1.result) | copy-start | bytes 737284

commit v6 on v5

--- a/solution.py
+++ b/solution.py
@@ -315,12 +315,13 @@
             )
         )
     ]
-    for copy in inputs[:4] + loads + inputs[4:]:
-        copy.start()
+    inputs[0].start()
     barrier = pltpu.get_barrier_semaphore()
     greeted = plane_peers + line_peers + edge_peers + [y_peers[1], y_peers[3], (0, partner)]
     for _, to in greeted:
         pl.semaphore_signal(barrier, inc=1, device_id=to, device_id_type=MESH)
+    for copy in inputs[1:4] + loads + inputs[4:]:
+        copy.start()
 
     inputs[0].wait()
     places[...] = window_table(corners, ix, iz, iy, ik)

time: 45.2 us -> 45.2 us (level)
  no operation moved by 1% of the time
where the time goes in v6:
time: 45.2 us; the launch traced here: 45.1 us
  Pallas kernels  43.5 us (96%)
  local copies, waits for them, and re-layouts  0.94 us (2%)
  between operations  0.66 us (1%)
    pallas_call x1, Pallas kernels, on_device(): pl.pallas_call(exchange_kernel, out_shape=jax.ShapeDtypeStruct((3, SLOTS...  41.6 us
    pallas_call x1, Pallas kernels, on_device(): pl.pallas_call(place_kernel, out_shape=(jax.ShapeDtypeStruct(fine.shape,...  1.88 us
    unnamed x4, local copies, waits for them, and re-layouts  0.94 us

profile of v6, /device:TPU:8, one launch (start us, length us, event | category | flops | bytes accessed | tf_op | source)
XLA Modules:
  0.0 45.1 jit_solution(7595025923414232461)
XLA Ops:
  0.6 0.0 copy-start
  0.6 41.6 %exchange.1.result = f32[3,5,16,256]{3,2,1,0:T(8,128)} custom-call(s32[3,512]{1,0:T(4,128)} %bitcast.3, s32[1,512]{1,0:T(1,128)} %bitcast.5, s32[2,512]{1,0:T(2,128)} %bitcast.4, f32[3,32,32,256]{3,2,1,0:T(8,128)} %coarse.3, f32[3,4,16,256]{3,2,1,0:T(8,128)} %fine_in.1, f32[4,16,256]{2,1,0:T(8,128)} %visc_in.1, bf16[3,128,128]{2,1,0:T(8,128)(2,1)} %constant.12.clone.side_in, ...), custom_call_target="tpu_custom_call" | custom-call | tf_op jit(solution)/shard_map/exchange/pallas_call | solution.py:544
  42.2 0.0 copy-done
  42.2 0.0 copy-start.1
  42.3 0.9 %copy-done.1 = f32[3,5,16,256]{3,2,1,0:T(8,128)S(1)} copy-done((f32[3,5,16,256]{3,2,1,0:T(8,128)S(1)}, f32[3,5,16,256]{3,2,1,0:T(8,128)}, u32[]{:S(2)}) %copy-start.1) | copy-done | bytes 245784
  43.2 1.9 %place.1 = (f32[3,4,16,256]{3,2,1,0:T(8,128)}, f32[3,32,32,256]{3,2,1,0:T(8,128)}) custom-call(f32[3,5,16,256]{3,2,1,0:T(8,128)S(1)} %copy-done.1, f32[3,32,32,256]{3,2,1,0:T(8,128)S(1)} %copy-done), custom_call_target="tpu_custom_call" | custom-call | tf_op jit(solution)/shard_map/place/pallas_call | solution.py:582
Async XLA Ops:
  0.6 41.6 %copy-start = (f32[3,32,32,256]{3,2,1,0:T(8,128)S(1)}, f32[3,32,32,256]{3,2,1,0:T(8,128)}, u32[]{:S(2)}) copy-start(f32[3,32,32,256]{3,2,1,0:T(8,128)} %coarse.3) | copy-start | bytes 9437188
  42.2 0.9 %copy-start.1 = (f32[3,5,16,256]{3,2,1,0:T(8,128)S(1)}, f32[3,5,16,256]{3,2,1,0:T(8,128)}, u32[]{:S(2)}) copy-start(f32[3,5,16,256]{3,2,1,0:T(8,128)} %exchange.1.result) | copy-start | bytes 737284
